TPU v7x, 128 devices: a whole 4x4x4 slice. The times are simulated.
128 devices in a mesh: dp: 1, cols: 16 (over z, y), rows: 8 (over x, core).
Axes of the slice: x: 4, y: 4, z: 4, core: 2. Of those that a mesh axis runs over, the one named last changes fastest.
Arguments:
- h_init: bfloat16 [2, 96, 192, 384], P('dp', 'rows', 'cols')
- c_init: float32 [2, 96, 192, 384], P('dp', 'rows', 'cols')
- w_rec: bfloat16 [3, 3, 384, 1536], replicated
- gate_bias: float32 [12, 1536], replicated
Outputs:
- output 1: bfloat16 [12, 2, 96, 192, 384], P(None, 'dp', 'rows', 'cols')
- output 2: float32 [2, 96, 192, 384], P('dp', 'rows', 'cols')
All inputs are finite; a program needn't handle non-finite values.
Results may differ from a plain program's by a relative error of at most 0.00284197.
Values are sent between devices in bfloat16 or wider.
A program may use at most 1 GiB of HBM per device.

v0:
```python
import jax
import jax.numpy as jnp
from jax import lax
from jax.sharding import PartitionSpec as P


def lstm_update(gate_pre, c_prev):
    in_gate, forget_gate, out_gate, cand_gate = jnp.split(gate_pre, 4, axis=-1)
    c_next = jax.nn.sigmoid(forget_gate) * c_prev + jax.nn.sigmoid(in_gate) * jnp.tanh(cand_gate)
    h_next = (jax.nn.sigmoid(out_gate) * jnp.tanh(c_next)).astype(jnp.bfloat16)
    return h_next, c_next


def solution(mesh):
    row_count = mesh.shape["rows"]
    col_count = mesh.shape["cols"]
    rows_down = [(src_pos, src_pos + 1) for src_pos in range(row_count - 1)]
    rows_up = [(src_pos + 1, src_pos) for src_pos in range(row_count - 1)]
    cols_right = [(src_pos, src_pos + 1) for src_pos in range(col_count - 1)]
    cols_left = [(src_pos + 1, src_pos) for src_pos in range(col_count - 1)]

    def with_halo(tile):
        from_above = lax.ppermute(tile[:, -1:], "rows", rows_down)
        from_below = lax.ppermute(tile[:, :1], "rows", rows_up)
        tall_tile = jnp.concatenate([from_above, tile, from_below], axis=1)
        from_left = lax.ppermute(tall_tile[:, :, -1:], "cols", cols_right)
        from_right = lax.ppermute(tall_tile[:, :, :1], "cols", cols_left)
        return jnp.concatenate([from_left, tall_tile, from_right], axis=2)

    def device_fn(h_init, c_init, w_rec, gate_bias):
        def one_step(carry_in, bias_row):
            h_prev, c_prev = carry_in
            padded = with_halo(h_prev)
            gate_pre = lax.conv_general_dilated(padded, w_rec, (1, 1), "VALID", dimension_numbers=("NHWC", "HWIO", "NHWC"), preferred_element_type=jnp.float32) + bias_row
            h_next, c_next = lstm_update(gate_pre, c_prev)
            return (h_next, c_next), h_next

        final_state, h_seq = lax.scan(one_step, (h_init, c_init), gate_bias)
        return h_seq, final_state[1]

    state_spec = P("dp", "rows", "cols", None)
    return jax.shard_map(device_fn, mesh=mesh, in_specs=(state_spec, state_spec, P(), P()), out_specs=(P(None, "dp", "rows", "cols", None), state_spec), check_vma=False)
```

profile of v0, /device:TPU:97, one launch (start us, length us, event | category | flops | bytes accessed | tf_op | source)
XLA Modules:
  0.0 403.2 jit_solution(10294761250949693479)
XLA Ops:
  2.6 399.8 %while.14 = (s32[]{:T(128)}, bf16[2,12,12,384]{3,0,2,1:T(2,128)(2,1)S(1)}, f32[2,12,12,384]{3,0,2,1:T(2,128)S(1)}, bf16[12,2,12,12,384]{4,1,3,2,0:T(2,128)(2,1)}...) while((s32[]{:T(128)}, bf16[2,12,12,384]{3,0,2,1:T(2,128)(2,1)S(1)}, ...), condition=%wide.region_1.2_spmd, body=%wide.region_0.1_spmd.sunk | while | flops 3060541440 | bytes 16797948 | solution.py:38
  2.6 3.7 collective-permute-start
  11.4 4.5 %collective-permute-start.2 = (bf16[2,14,1,384]{3,0,2,1:T(2,128)(2,1)S(1)}, bf16[2,14,1,384]{3,0,2,1:T(2,128)(2,1)S(1)}, u32[]{:S(2)}, u32[]{:S(2)}) collective-permute-start(bf16[2,14,1,384]{3,0,2,1:T(2,128)(2,1)S(1)} %get-tuple-element.102), channel_id=1, source_target_pairs={{8,0},{16,8},{24,16},{32,24},{40,32},{48,40},{56,48},{64,56},{72,6... | collective-permute-start | bytes 64520 | tf_op jit(solution)/shard_map/while/body/eval_jaxpr/ppermute | solution.py:27
  18.7 3.9 collective-permute-done.3
  22.6 13.6 %convolution_add_fusion.2 = f32[2,12,12,1536]{3,0,2,1:T(2,128)S(1)} fusion(bf16[3,3,384,1536]{3,2,1,0:T(8,128)(2,1)} %get-tuple-element.125, f32[1536]{0:T(1024)S(1)} %dynamic-slice_reduce_fusion.2, bf16[2,14,1,384]{3,0,2,1:T(2,128)(2,1)S(1)} %collective-permute-done.2, bf16[2,14,12,384]{3,0,2,1:T(2,128)(2,1)S(1)} %constant_dynamic-update-slice_fusion.8, ...), kind=kOutput, calls=%fused_computation.clone.1 | convolution fusion | flops 3058993152 | bytes 12693504 | tf_op jit(solution)/shard_map/while/body/eval_jaxpr/conv_general_dilated | solution.py:34
  38.8 3.4 collective-permute-start
  49.2 3.4 collective-permute-start.3
  55.9 13.6 %convolution_add_fusion.2 = f32[2,12,12,1536]{3,0,2,1:T(2,128)S(1)} fusion(bf16[3,3,384,1536]{3,2,1,0:T(8,128)(2,1)} %get-tuple-element.125, f32[1536]{0:T(1024)S(1)} %dynamic-slice_reduce_fusion.2, bf16[2,14,1,384]{3,0,2,1:T(2,128)(2,1)S(1)} %collective-permute-done.2, bf16[2,14,12,384]{3,0,2,1:T(2,128)(2,1)S(1)} %constant_dynamic-update-slice_fusion.8, ...), kind=kOutput, calls=%fused_computation.clone.1 | convolution fusion | flops 3058993152 | bytes 12693504 | tf_op jit(solution)/shard_map/while/body/eval_jaxpr/conv_general_dilated | solution.py:34
  72.1 3.1 collective-permute-start
  82.3 3.4 collective-permute-start.3
  88.9 13.6 %convolution_add_fusion.2 = f32[2,12,12,1536]{3,0,2,1:T(2,128)S(1)} fusion(bf16[3,3,384,1536]{3,2,1,0:T(8,128)(2,1)} %get-tuple-element.125, f32[1536]{0:T(1024)S(1)} %dynamic-slice_reduce_fusion.2, bf16[2,14,1,384]{3,0,2,1:T(2,128)(2,1)S(1)} %collective-permute-done.2, bf16[2,14,12,384]{3,0,2,1:T(2,128)(2,1)S(1)} %constant_dynamic-update-slice_fusion.8, ...), kind=kOutput, calls=%fused_computation.clone.1 | convolution fusion | flops 3058993152 | bytes 12693504 | tf_op jit(solution)/shard_map/while/body/eval_jaxpr/conv_general_dilated | solution.py:34
  105.1 3.1 collective-permute-start
  115.3 3.4 collective-permute-start.3
  122.0 13.6 %convolution_add_fusion.2 = f32[2,12,12,1536]{3,0,2,1:T(2,128)S(1)} fusion(bf16[3,3,384,1536]{3,2,1,0:T(8,128)(2,1)} %get-tuple-element.125, f32[1536]{0:T(1024)S(1)} %dynamic-slice_reduce_fusion.2, bf16[2,14,1,384]{3,0,2,1:T(2,128)(2,1)S(1)} %collective-permute-done.2, bf16[2,14,12,384]{3,0,2,1:T(2,128)(2,1)S(1)} %constant_dynamic-update-slice_fusion.8, ...), kind=kOutput, calls=%fused_computation.clone.1 | convolution fusion | flops 3058993152 | bytes 12693504 | tf_op jit(solution)/shard_map/while/body/eval_jaxpr/conv_general_dilated | solution.py:34
  138.2 3.1 collective-permute-start
  148.3 3.4 collective-permute-start.3
  155.0 13.6 %convolution_add_fusion.2 = f32[2,12,12,1536]{3,0,2,1:T(2,128)S(1)} fusion(bf16[3,3,384,1536]{3,2,1,0:T(8,128)(2,1)} %get-tuple-element.125, f32[1536]{0:T(1024)S(1)} %dynamic-slice_reduce_fusion.2, bf16[2,14,1,384]{3,0,2,1:T(2,128)(2,1)S(1)} %collective-permute-done.2, bf16[2,14,12,384]{3,0,2,1:T(2,128)(2,1)S(1)} %constant_dynamic-update-slice_fusion.8, ...), kind=kOutput, calls=%fused_computation.clone.1 | convolution fusion | flops 3058993152 | bytes 12693504 | tf_op jit(solution)/shard_map/while/body/eval_jaxpr/conv_general_dilated | solution.py:34
  181.4 3.4 collective-permute-start.3
  188.0 13.6 %convolution_add_fusion.2 = f32[2,12,12,1536]{3,0,2,1:T(2,128)S(1)} fusion(bf16[3,3,384,1536]{3,2,1,0:T(8,128)(2,1)} %get-tuple-element.125, f32[1536]{0:T(1024)S(1)} %dynamic-slice_reduce_fusion.2, bf16[2,14,1,384]{3,0,2,1:T(2,128)(2,1)S(1)} %collective-permute-done.2, bf16[2,14,12,384]{3,0,2,1:T(2,128)(2,1)S(1)} %constant_dynamic-update-slice_fusion.8, ...), kind=kOutput, calls=%fused_computation.clone.1 | convolution fusion | flops 3058993152 | bytes 12693504 | tf_op jit(solution)/shard_map/while/body/eval_jaxpr/conv_general_dilated | solution.py:34
  214.4 3.4 collective-permute-start.3
  221.1 13.6 %convolution_add_fusion.2 = f32[2,12,12,1536]{3,0,2,1:T(2,128)S(1)} fusion(bf16[3,3,384,1536]{3,2,1,0:T(8,128)(2,1)} %get-tuple-element.125, f32[1536]{0:T(1024)S(1)} %dynamic-slice_reduce_fusion.2, bf16[2,14,1,384]{3,0,2,1:T(2,128)(2,1)S(1)} %collective-permute-done.2, bf16[2,14,12,384]{3,0,2,1:T(2,128)(2,1)S(1)} %constant_dynamic-update-slice_fusion.8, ...), kind=kOutput, calls=%fused_computation.clone.1 | convolution fusion | flops 3058993152 | bytes 12693504 | tf_op jit(solution)/shard_map/while/body/eval_jaxpr/conv_general_dilated | solution.py:34
  247.4 3.4 collective-permute-start.3
  254.1 13.6 %convolution_add_fusion.2 = f32[2,12,12,1536]{3,0,2,1:T(2,128)S(1)} fusion(bf16[3,3,384,1536]{3,2,1,0:T(8,128)(2,1)} %get-tuple-element.125, f32[1536]{0:T(1024)S(1)} %dynamic-slice_reduce_fusion.2, bf16[2,14,1,384]{3,0,2,1:T(2,128)(2,1)S(1)} %collective-permute-done.2, bf16[2,14,12,384]{3,0,2,1:T(2,128)(2,1)S(1)} %constant_dynamic-update-slice_fusion.8, ...), kind=kOutput, calls=%fused_computation.clone.1 | convolution fusion | flops 3058993152 | bytes 12693504 | tf_op jit(solution)/shard_map/while/body/eval_jaxpr/conv_general_dilated | solution.py:34
  280.5 3.4 collective-permute-start.3
  287.1 13.6 %convolution_add_fusion.2 = f32[2,12,12,1536]{3,0,2,1:T(2,128)S(1)} fusion(bf16[3,3,384,1536]{3,2,1,0:T(8,128)(2,1)} %get-tuple-element.125, f32[1536]{0:T(1024)S(1)} %dynamic-slice_reduce_fusion.2, bf16[2,14,1,384]{3,0,2,1:T(2,128)(2,1)S(1)} %collective-permute-done.2, bf16[2,14,12,384]{3,0,2,1:T(2,128)(2,1)S(1)} %constant_dynamic-update-slice_fusion.8, ...), kind=kOutput, calls=%fused_computation.clone.1 | convolution fusion | flops 3058993152 | bytes 12693504 | tf_op jit(solution)/shard_map/while/body/eval_jaxpr/conv_general_dilated | solution.py:34
  313.5 3.4 collective-permute-start.3
  320.1 13.6 %convolution_add_fusion.2 = f32[2,12,12,1536]{3,0,2,1:T(2,128)S(1)} fusion(bf16[3,3,384,1536]{3,2,1,0:T(8,128)(2,1)} %get-tuple-element.125, f32[1536]{0:T(1024)S(1)} %dynamic-slice_reduce_fusion.2, bf16[2,14,1,384]{3,0,2,1:T(2,128)(2,1)S(1)} %collective-permute-done.2, bf16[2,14,12,384]{3,0,2,1:T(2,128)(2,1)S(1)} %constant_dynamic-update-slice_fusion.8, ...), kind=kOutput, calls=%fused_computation.clone.1 | convolution fusion | flops 3058993152 | bytes 12693504 | tf_op jit(solution)/shard_map/while/body/eval_jaxpr/conv_general_dilated | solution.py:34
  346.5 3.4 collective-permute-start.3
  353.2 13.6 %convolution_add_fusion.2 = f32[2,12,12,1536]{3,0,2,1:T(2,128)S(1)} fusion(bf16[3,3,384,1536]{3,2,1,0:T(8,128)(2,1)} %get-tuple-element.125, f32[1536]{0:T(1024)S(1)} %dynamic-slice_reduce_fusion.2, bf16[2,14,1,384]{3,0,2,1:T(2,128)(2,1)S(1)} %collective-permute-done.2, bf16[2,14,12,384]{3,0,2,1:T(2,128)(2,1)S(1)} %constant_dynamic-update-slice_fusion.8, ...), kind=kOutput, calls=%fused_computation.clone.1 | convolution fusion | flops 3058993152 | bytes 12693504 | tf_op jit(solution)/shard_map/while/body/eval_jaxpr/conv_general_dilated | solution.py:34
  369.4 3.1 collective-permute-start
  379.6 3.4 collective-permute-start.3
  386.2 13.6 %convolution_add_fusion.2 = f32[2,12,12,1536]{3,0,2,1:T(2,128)S(1)} fusion(bf16[3,3,384,1536]{3,2,1,0:T(8,128)(2,1)} %get-tuple-element.125, f32[1536]{0:T(1024)S(1)} %dynamic-slice_reduce_fusion.2, bf16[2,14,1,384]{3,0,2,1:T(2,128)(2,1)S(1)} %collective-permute-done.2, bf16[2,14,12,384]{3,0,2,1:T(2,128)(2,1)S(1)} %constant_dynamic-update-slice_fusion.8, ...), kind=kOutput, calls=%fused_computation.clone.1 | convolution fusion | flops 3058993152 | bytes 12693504 | tf_op jit(solution)/shard_map/while/body/eval_jaxpr/conv_general_dilated | solution.py:34
  (166 shorter events, 173.5 us)
Async XLA Ops:
  2.6 5.6 %collective-permute-start = (bf16[2,1,12,384]{3,0,2,1:T(2,128)(2,1)S(1)}, bf16[2,1,12,384]{3,0,2,1:T(2,128)(2,1)S(1)}, u32[]{:S(2)}, u32[]{:S(2)}) collective-permute-start(bf16[2,1,12,384]{3,0,2,1:T(2,128)(2,1)S(1)} %get-tuple-element.100), channel_id=1, source_target_pairs={{0,1},{1,2},{2,3},{3,4},{4,5},{5,6},{6,7},{8,9},{9,10},{10,11},{11... | collective-permute-start | bytes 55304 | tf_op jit(solution)/shard_map/while/body/eval_jaxpr/ppermute | solution.py:23
  6.3 5.1 %collective-permute-start.1 = (bf16[2,1,12,384]{3,0,2,1:T(2,128)(2,1)S(1)}, bf16[2,1,12,384]{3,0,2,1:T(2,128)(2,1)S(1)}, u32[]{:S(2)}, u32[]{:S(2)}) collective-permute-start(bf16[2,1,12,384]{3,0,2,1:T(2,128)(2,1)S(1)} %get-tuple-element.101), channel_id=1, source_target_pairs={{1,0},{2,1},{3,2},{4,3},{5,4},{6,5},{7,6},{9,8},{10,9},{11,10},{12... | collective-permute-start | bytes 55304 | tf_op jit(solution)/shard_map/while/body/eval_jaxpr/ppermute | solution.py:24
  11.4 7.2 %collective-permute-start.2 = (bf16[2,14,1,384]{3,0,2,1:T(2,128)(2,1)S(1)}, bf16[2,14,1,384]{3,0,2,1:T(2,128)(2,1)S(1)}, u32[]{:S(2)}, u32[]{:S(2)}) collective-permute-start(bf16[2,14,1,384]{3,0,2,1:T(2,128)(2,1)S(1)} %get-tuple-element.102), channel_id=1, source_target_pairs={{8,0},{16,8},{24,16},{32,24},{40,32},{48,40},{56,48},{64,56},{72,6... | collective-permute-start | bytes 64520 | tf_op jit(solution)/shard_map/while/body/eval_jaxpr/ppermute | solution.py:27
  15.9 6.6 %collective-permute-start.3 = (bf16[2,14,1,384]{3,0,2,1:T(2,128)(2,1)S(1)}, bf16[2,14,1,384]{3,0,2,1:T(2,128)(2,1)S(1)}, u32[]{:S(2)}, u32[]{:S(2)}) collective-permute-start(bf16[2,14,1,384]{3,0,2,1:T(2,128)(2,1)S(1)} %get-tuple-element.103), channel_id=1, source_target_pairs={{0,8},{8,16},{16,24},{24,32},{32,40},{40,48},{48,56},{56,64},{64,7... | collective-permute-start | bytes 64520 | tf_op jit(solution)/shard_map/while/body/eval_jaxpr/ppermute | solution.py:26
  38.8 5.3 %collective-permute-start = (bf16[2,1,12,384]{3,0,2,1:T(2,128)(2,1)S(1)}, bf16[2,1,12,384]{3,0,2,1:T(2,128)(2,1)S(1)}, u32[]{:S(2)}, u32[]{:S(2)}) collective-permute-start(bf16[2,1,12,384]{3,0,2,1:T(2,128)(2,1)S(1)} %get-tuple-element.100), channel_id=1, source_target_pairs={{0,1},{1,2},{2,3},{3,4},{4,5},{5,6},{6,7},{8,9},{9,10},{10,11},{11... | collective-permute-start | bytes 55304 | tf_op jit(solution)/shard_map/while/body/eval_jaxpr/ppermute | solution.py:23
  42.2 5.1 %collective-permute-start.1 = (bf16[2,1,12,384]{3,0,2,1:T(2,128)(2,1)S(1)}, bf16[2,1,12,384]{3,0,2,1:T(2,128)(2,1)S(1)}, u32[]{:S(2)}, u32[]{:S(2)}) collective-permute-start(bf16[2,1,12,384]{3,0,2,1:T(2,128)(2,1)S(1)} %get-tuple-element.101), channel_id=1, source_target_pairs={{1,0},{2,1},{3,2},{4,3},{5,4},{6,5},{7,6},{9,8},{10,9},{11,10},{12... | collective-permute-start | bytes 55304 | tf_op jit(solution)/shard_map/while/body/eval_jaxpr/ppermute | solution.py:24
  47.3 6.1 %collective-permute-start.2 = (bf16[2,14,1,384]{3,0,2,1:T(2,128)(2,1)S(1)}, bf16[2,14,1,384]{3,0,2,1:T(2,128)(2,1)S(1)}, u32[]{:S(2)}, u32[]{:S(2)}) collective-permute-start(bf16[2,14,1,384]{3,0,2,1:T(2,128)(2,1)S(1)} %get-tuple-element.102), channel_id=1, source_target_pairs={{8,0},{16,8},{24,16},{32,24},{40,32},{48,40},{56,48},{64,56},{72,6... | collective-permute-start | bytes 64520 | tf_op jit(solution)/shard_map/while/body/eval_jaxpr/ppermute | solution.py:27
  49.2 6.6 %collective-permute-start.3 = (bf16[2,14,1,384]{3,0,2,1:T(2,128)(2,1)S(1)}, bf16[2,14,1,384]{3,0,2,1:T(2,128)(2,1)S(1)}, u32[]{:S(2)}, u32[]{:S(2)}) collective-permute-start(bf16[2,14,1,384]{3,0,2,1:T(2,128)(2,1)S(1)} %get-tuple-element.103), channel_id=1, source_target_pairs={{0,8},{8,16},{16,24},{24,32},{32,40},{40,48},{48,56},{56,64},{64,7... | collective-permute-start | bytes 64520 | tf_op jit(solution)/shard_map/while/body/eval_jaxpr/ppermute | solution.py:26
  75.2 5.1 %collective-permute-start.1 = (bf16[2,1,12,384]{3,0,2,1:T(2,128)(2,1)S(1)}, bf16[2,1,12,384]{3,0,2,1:T(2,128)(2,1)S(1)}, u32[]{:S(2)}, u32[]{:S(2)}) collective-permute-start(bf16[2,1,12,384]{3,0,2,1:T(2,128)(2,1)S(1)} %get-tuple-element.101), channel_id=1, source_target_pairs={{1,0},{2,1},{3,2},{4,3},{5,4},{6,5},{7,6},{9,8},{10,9},{11,10},{12... | collective-permute-start | bytes 55304 | tf_op jit(solution)/shard_map/while/body/eval_jaxpr/ppermute | solution.py:24
  80.3 6.1 %collective-permute-start.2 = (bf16[2,14,1,384]{3,0,2,1:T(2,128)(2,1)S(1)}, bf16[2,14,1,384]{3,0,2,1:T(2,128)(2,1)S(1)}, u32[]{:S(2)}, u32[]{:S(2)}) collective-permute-start(bf16[2,14,1,384]{3,0,2,1:T(2,128)(2,1)S(1)} %get-tuple-element.102), channel_id=1, source_target_pairs={{8,0},{16,8},{24,16},{32,24},{40,32},{48,40},{56,48},{64,56},{72,6... | collective-permute-start | bytes 64520 | tf_op jit(solution)/shard_map/while/body/eval_jaxpr/ppermute | solution.py:27
  82.3 6.6 %collective-permute-start.3 = (bf16[2,14,1,384]{3,0,2,1:T(2,128)(2,1)S(1)}, bf16[2,14,1,384]{3,0,2,1:T(2,128)(2,1)S(1)}, u32[]{:S(2)}, u32[]{:S(2)}) collective-permute-start(bf16[2,14,1,384]{3,0,2,1:T(2,128)(2,1)S(1)} %get-tuple-element.103), channel_id=1, source_target_pairs={{0,8},{8,16},{16,24},{24,32},{32,40},{40,48},{48,56},{56,64},{64,7... | collective-permute-start | bytes 64520 | tf_op jit(solution)/shard_map/while/body/eval_jaxpr/ppermute | solution.py:26
  108.2 5.1 %collective-permute-start.1 = (bf16[2,1,12,384]{3,0,2,1:T(2,128)(2,1)S(1)}, bf16[2,1,12,384]{3,0,2,1:T(2,128)(2,1)S(1)}, u32[]{:S(2)}, u32[]{:S(2)}) collective-permute-start(bf16[2,1,12,384]{3,0,2,1:T(2,128)(2,1)S(1)} %get-tuple-element.101), channel_id=1, source_target_pairs={{1,0},{2,1},{3,2},{4,3},{5,4},{6,5},{7,6},{9,8},{10,9},{11,10},{12... | collective-permute-start | bytes 55304 | tf_op jit(solution)/shard_map/while/body/eval_jaxpr/ppermute | solution.py:24
  113.4 6.1 %collective-permute-start.2 = (bf16[2,14,1,384]{3,0,2,1:T(2,128)(2,1)S(1)}, bf16[2,14,1,384]{3,0,2,1:T(2,128)(2,1)S(1)}, u32[]{:S(2)}, u32[]{:S(2)}) collective-permute-start(bf16[2,14,1,384]{3,0,2,1:T(2,128)(2,1)S(1)} %get-tuple-element.102), channel_id=1, source_target_pairs={{8,0},{16,8},{24,16},{32,24},{40,32},{48,40},{56,48},{64,56},{72,6... | collective-permute-start | bytes 64520 | tf_op jit(solution)/shard_map/while/body/eval_jaxpr/ppermute | solution.py:27
  115.3 6.6 %collective-permute-start.3 = (bf16[2,14,1,384]{3,0,2,1:T(2,128)(2,1)S(1)}, bf16[2,14,1,384]{3,0,2,1:T(2,128)(2,1)S(1)}, u32[]{:S(2)}, u32[]{:S(2)}) collective-permute-start(bf16[2,14,1,384]{3,0,2,1:T(2,128)(2,1)S(1)} %get-tuple-element.103), channel_id=1, source_target_pairs={{0,8},{8,16},{16,24},{24,32},{32,40},{40,48},{48,56},{56,64},{64,7... | collective-permute-start | bytes 64520 | tf_op jit(solution)/shard_map/while/body/eval_jaxpr/ppermute | solution.py:26
  141.3 5.1 %collective-permute-start.1 = (bf16[2,1,12,384]{3,0,2,1:T(2,128)(2,1)S(1)}, bf16[2,1,12,384]{3,0,2,1:T(2,128)(2,1)S(1)}, u32[]{:S(2)}, u32[]{:S(2)}) collective-permute-start(bf16[2,1,12,384]{3,0,2,1:T(2,128)(2,1)S(1)} %get-tuple-element.101), channel_id=1, source_target_pairs={{1,0},{2,1},{3,2},{4,3},{5,4},{6,5},{7,6},{9,8},{10,9},{11,10},{12... | collective-permute-start | bytes 55304 | tf_op jit(solution)/shard_map/while/body/eval_jaxpr/ppermute | solution.py:24
  146.4 6.1 %collective-permute-start.2 = (bf16[2,14,1,384]{3,0,2,1:T(2,128)(2,1)S(1)}, bf16[2,14,1,384]{3,0,2,1:T(2,128)(2,1)S(1)}, u32[]{:S(2)}, u32[]{:S(2)}) collective-permute-start(bf16[2,14,1,384]{3,0,2,1:T(2,128)(2,1)S(1)} %get-tuple-element.102), channel_id=1, source_target_pairs={{8,0},{16,8},{24,16},{32,24},{40,32},{48,40},{56,48},{64,56},{72,6... | collective-permute-start | bytes 64520 | tf_op jit(solution)/shard_map/while/body/eval_jaxpr/ppermute | solution.py:27
  148.3 6.6 %collective-permute-start.3 = (bf16[2,14,1,384]{3,0,2,1:T(2,128)(2,1)S(1)}, bf16[2,14,1,384]{3,0,2,1:T(2,128)(2,1)S(1)}, u32[]{:S(2)}, u32[]{:S(2)}) collective-permute-start(bf16[2,14,1,384]{3,0,2,1:T(2,128)(2,1)S(1)} %get-tuple-element.103), channel_id=1, source_target_pairs={{0,8},{8,16},{16,24},{24,32},{32,40},{40,48},{48,56},{56,64},{64,7... | collective-permute-start | bytes 64520 | tf_op jit(solution)/shard_map/while/body/eval_jaxpr/ppermute | solution.py:26
  174.3 5.1 %collective-permute-start.1 = (bf16[2,1,12,384]{3,0,2,1:T(2,128)(2,1)S(1)}, bf16[2,1,12,384]{3,0,2,1:T(2,128)(2,1)S(1)}, u32[]{:S(2)}, u32[]{:S(2)}) collective-permute-start(bf16[2,1,12,384]{3,0,2,1:T(2,128)(2,1)S(1)} %get-tuple-element.101), channel_id=1, source_target_pairs={{1,0},{2,1},{3,2},{4,3},{5,4},{6,5},{7,6},{9,8},{10,9},{11,10},{12... | collective-permute-start | bytes 55304 | tf_op jit(solution)/shard_map/while/body/eval_jaxpr/ppermute | solution.py:24
  179.4 6.1 %collective-permute-start.2 = (bf16[2,14,1,384]{3,0,2,1:T(2,128)(2,1)S(1)}, bf16[2,14,1,384]{3,0,2,1:T(2,128)(2,1)S(1)}, u32[]{:S(2)}, u32[]{:S(2)}) collective-permute-start(bf16[2,14,1,384]{3,0,2,1:T(2,128)(2,1)S(1)} %get-tuple-element.102), channel_id=1, source_target_pairs={{8,0},{16,8},{24,16},{32,24},{40,32},{48,40},{56,48},{64,56},{72,6... | collective-permute-start | bytes 64520 | tf_op jit(solution)/shard_map/while/body/eval_jaxpr/ppermute | solution.py:27
  181.4 6.6 %collective-permute-start.3 = (bf16[2,14,1,384]{3,0,2,1:T(2,128)(2,1)S(1)}, bf16[2,14,1,384]{3,0,2,1:T(2,128)(2,1)S(1)}, u32[]{:S(2)}, u32[]{:S(2)}) collective-permute-start(bf16[2,14,1,384]{3,0,2,1:T(2,128)(2,1)S(1)} %get-tuple-element.103), channel_id=1, source_target_pairs={{0,8},{8,16},{16,24},{24,32},{32,40},{40,48},{48,56},{56,64},{64,7... | collective-permute-start | bytes 64520 | tf_op jit(solution)/shard_map/while/body/eval_jaxpr/ppermute | solution.py:26
  212.5 6.1 %collective-permute-start.2 = (bf16[2,14,1,384]{3,0,2,1:T(2,128)(2,1)S(1)}, bf16[2,14,1,384]{3,0,2,1:T(2,128)(2,1)S(1)}, u32[]{:S(2)}, u32[]{:S(2)}) collective-permute-start(bf16[2,14,1,384]{3,0,2,1:T(2,128)(2,1)S(1)} %get-tuple-element.102), channel_id=1, source_target_pairs={{8,0},{16,8},{24,16},{32,24},{40,32},{48,40},{56,48},{64,56},{72,6... | collective-permute-start | bytes 64520 | tf_op jit(solution)/shard_map/while/body/eval_jaxpr/ppermute | solution.py:27
  214.4 6.6 %collective-permute-start.3 = (bf16[2,14,1,384]{3,0,2,1:T(2,128)(2,1)S(1)}, bf16[2,14,1,384]{3,0,2,1:T(2,128)(2,1)S(1)}, u32[]{:S(2)}, u32[]{:S(2)}) collective-permute-start(bf16[2,14,1,384]{3,0,2,1:T(2,128)(2,1)S(1)} %get-tuple-element.103), channel_id=1, source_target_pairs={{0,8},{8,16},{16,24},{24,32},{32,40},{40,48},{48,56},{56,64},{64,7... | collective-permute-start | bytes 64520 | tf_op jit(solution)/shard_map/while/body/eval_jaxpr/ppermute | solution.py:26
  245.5 6.1 %collective-permute-start.2 = (bf16[2,14,1,384]{3,0,2,1:T(2,128)(2,1)S(1)}, bf16[2,14,1,384]{3,0,2,1:T(2,128)(2,1)S(1)}, u32[]{:S(2)}, u32[]{:S(2)}) collective-permute-start(bf16[2,14,1,384]{3,0,2,1:T(2,128)(2,1)S(1)} %get-tuple-element.102), channel_id=1, source_target_pairs={{8,0},{16,8},{24,16},{32,24},{40,32},{48,40},{56,48},{64,56},{72,6... | collective-permute-start | bytes 64520 | tf_op jit(solution)/shard_map/while/body/eval_jaxpr/ppermute | solution.py:27
  247.4 6.6 %collective-permute-start.3 = (bf16[2,14,1,384]{3,0,2,1:T(2,128)(2,1)S(1)}, bf16[2,14,1,384]{3,0,2,1:T(2,128)(2,1)S(1)}, u32[]{:S(2)}, u32[]{:S(2)}) collective-permute-start(bf16[2,14,1,384]{3,0,2,1:T(2,128)(2,1)S(1)} %get-tuple-element.103), channel_id=1, source_target_pairs={{0,8},{8,16},{16,24},{24,32},{32,40},{40,48},{48,56},{56,64},{64,7... | collective-permute-start | bytes 64520 | tf_op jit(solution)/shard_map/while/body/eval_jaxpr/ppermute | solution.py:26
  278.5 6.1 %collective-permute-start.2 = (bf16[2,14,1,384]{3,0,2,1:T(2,128)(2,1)S(1)}, bf16[2,14,1,384]{3,0,2,1:T(2,128)(2,1)S(1)}, u32[]{:S(2)}, u32[]{:S(2)}) collective-permute-start(bf16[2,14,1,384]{3,0,2,1:T(2,128)(2,1)S(1)} %get-tuple-element.102), channel_id=1, source_target_pairs={{8,0},{16,8},{24,16},{32,24},{40,32},{48,40},{56,48},{64,56},{72,6... | collective-permute-start | bytes 64520 | tf_op jit(solution)/shard_map/while/body/eval_jaxpr/ppermute | solution.py:27
  280.5 6.6 %collective-permute-start.3 = (bf16[2,14,1,384]{3,0,2,1:T(2,128)(2,1)S(1)}, bf16[2,14,1,384]{3,0,2,1:T(2,128)(2,1)S(1)}, u32[]{:S(2)}, u32[]{:S(2)}) collective-permute-start(bf16[2,14,1,384]{3,0,2,1:T(2,128)(2,1)S(1)} %get-tuple-element.103), channel_id=1, source_target_pairs={{0,8},{8,16},{16,24},{24,32},{32,40},{40,48},{48,56},{56,64},{64,7... | collective-permute-start | bytes 64520 | tf_op jit(solution)/shard_map/while/body/eval_jaxpr/ppermute | solution.py:26
  311.6 6.1 %collective-permute-start.2 = (bf16[2,14,1,384]{3,0,2,1:T(2,128)(2,1)S(1)}, bf16[2,14,1,384]{3,0,2,1:T(2,128)(2,1)S(1)}, u32[]{:S(2)}, u32[]{:S(2)}) collective-permute-start(bf16[2,14,1,384]{3,0,2,1:T(2,128)(2,1)S(1)} %get-tuple-element.102), channel_id=1, source_target_pairs={{8,0},{16,8},{24,16},{32,24},{40,32},{48,40},{56,48},{64,56},{72,6... | collective-permute-start | bytes 64520 | tf_op jit(solution)/shard_map/while/body/eval_jaxpr/ppermute | solution.py:27
  313.5 6.6 %collective-permute-start.3 = (bf16[2,14,1,384]{3,0,2,1:T(2,128)(2,1)S(1)}, bf16[2,14,1,384]{3,0,2,1:T(2,128)(2,1)S(1)}, u32[]{:S(2)}, u32[]{:S(2)}) collective-permute-start(bf16[2,14,1,384]{3,0,2,1:T(2,128)(2,1)S(1)} %get-tuple-element.103), channel_id=1, source_target_pairs={{0,8},{8,16},{16,24},{24,32},{32,40},{40,48},{48,56},{56,64},{64,7... | collective-permute-start | bytes 64520 | tf_op jit(solution)/shard_map/while/body/eval_jaxpr/ppermute | solution.py:26
  344.6 6.1 %collective-permute-start.2 = (bf16[2,14,1,384]{3,0,2,1:T(2,128)(2,1)S(1)}, bf16[2,14,1,384]{3,0,2,1:T(2,128)(2,1)S(1)}, u32[]{:S(2)}, u32[]{:S(2)}) collective-permute-start(bf16[2,14,1,384]{3,0,2,1:T(2,128)(2,1)S(1)} %get-tuple-element.102), channel_id=1, source_target_pairs={{8,0},{16,8},{24,16},{32,24},{40,32},{48,40},{56,48},{64,56},{72,6... | collective-permute-start | bytes 64520 | tf_op jit(solution)/shard_map/while/body/eval_jaxpr/ppermute | solution.py:27
  346.5 6.6 %collective-permute-start.3 = (bf16[2,14,1,384]{3,0,2,1:T(2,128)(2,1)S(1)}, bf16[2,14,1,384]{3,0,2,1:T(2,128)(2,1)S(1)}, u32[]{:S(2)}, u32[]{:S(2)}) collective-permute-start(bf16[2,14,1,384]{3,0,2,1:T(2,128)(2,1)S(1)} %get-tuple-element.103), channel_id=1, source_target_pairs={{0,8},{8,16},{16,24},{24,32},{32,40},{40,48},{48,56},{56,64},{64,7... | collective-permute-start | bytes 64520 | tf_op jit(solution)/shard_map/while/body/eval_jaxpr/ppermute | solution.py:26
  377.6 6.1 %collective-permute-start.2 = (bf16[2,14,1,384]{3,0,2,1:T(2,128)(2,1)S(1)}, bf16[2,14,1,384]{3,0,2,1:T(2,128)(2,1)S(1)}, u32[]{:S(2)}, u32[]{:S(2)}) collective-permute-start(bf16[2,14,1,384]{3,0,2,1:T(2,128)(2,1)S(1)} %get-tuple-element.102), channel_id=1, source_target_pairs={{8,0},{16,8},{24,16},{32,24},{40,32},{48,40},{56,48},{64,56},{72,6... | collective-permute-start | bytes 64520 | tf_op jit(solution)/shard_map/while/body/eval_jaxpr/ppermute | solution.py:27
  379.6 6.6 %collective-permute-start.3 = (bf16[2,14,1,384]{3,0,2,1:T(2,128)(2,1)S(1)}, bf16[2,14,1,384]{3,0,2,1:T(2,128)(2,1)S(1)}, u32[]{:S(2)}, u32[]{:S(2)}) collective-permute-start(bf16[2,14,1,384]{3,0,2,1:T(2,128)(2,1)S(1)} %get-tuple-element.103), channel_id=1, source_target_pairs={{0,8},{8,16},{16,24},{24,32},{32,40},{40,48},{48,56},{56,64},{64,7... | collective-permute-start | bytes 64520 | tf_op jit(solution)/shard_map/while/body/eval_jaxpr/ppermute | solution.py:26
  (17 other events, 81.4 us)
where the time goes:
time: 406 us; the launch traced here: 403 us
  matrix products  163 us (40%)
  starting transfers between devices  125 us (31%)
  waiting for transfers between devices  65.6 us (16%)
  other arithmetic  31 us (8%)
  local copies, waits for them, and re-layouts  16.2 us (4%)
    conv_general_dilated x12, matrix products, one_step(): lax.conv_general_dilated(padded, w_rec, (1, 1), 'VALID', dimension_number...  163 us
    ppermute x12, starting transfers between devices, with_halo(): from_left = lax.ppermute(tall_tile[:, :, -1:], 'cols', cols_right)  38.9 us
    ppermute x12, starting transfers between devices, with_halo(): from_above = lax.ppermute(tile[:, -1:], 'rows', rows_down)  37.8 us
    ppermute x12, waiting for transfers between devices, with_halo(): from_below = lax.ppermute(tile[:, :1], 'rows', rows_up)  34.9 us
    dynamic_update_slice x12, other arithmetic, device_fn(): final_state, h_seq = lax.scan(one_step, (h_init, c_init), gate_bias)  31 us
    ppermute x12, waiting for transfers between devices, with_halo(): from_left = lax.ppermute(tall_tile[:, :, -1:], 'cols', cols_right)  30.7 us
    ppermute x12, starting transfers between devices, with_halo(): from_right = lax.ppermute(tall_tile[:, :, :1], 'cols', cols_left)  25.6 us
    ppermute x12, starting transfers between devices, with_halo(): from_below = lax.ppermute(tile[:, :1], 'rows', rows_up)  23 us
  transfers between devices with their start and end apart: 48, of which 24 were waited for; matrix products, arithmetic and copies ran while one was open for 3% of the time, Pallas kernels for 0%

commit v1 on v0

v1 whole, which is shorter than its diff:
```python
import functools

import jax
import jax.numpy as jnp
from jax import lax
from jax.experimental import pallas as pl
from jax.experimental.pallas import tpu as pltpu
from jax.sharding import PartitionSpec as P

MESH = pl.DeviceIdType.MESH
STEPS = 12
S = 2
T = 12
LANES = 128
CH = 3
CDIM = CH * LANES
TAPS = 9
PITCH = 16
GROWS = 20 * PITCH
SLOTS = 4

DIRS = ((-1, 0), (1, 0), (0, -1), (0, 1), (-1, -1), (-1, 1), (1, -1), (1, 1))


def opposite(d):
    dy, dx = DIRS[d]
    return DIRS.index((-dy, -dx))


def at(y, x):
    return (y + 2) * PITCH + x + 2


def sigmoid(v):
    return 0.5 * jnp.tanh(0.5 * v) + 0.5


def lstm(gates, c_prev):
    i, f, o, g = (gates[:, k * LANES : (k + 1) * LANES] for k in range(4))
    c = sigmoid(f) * c_prev + sigmoid(i) * jnp.tanh(g)
    h = (sigmoid(o) * jnp.tanh(c)).astype(jnp.bfloat16)
    return h, c


def gather_tile(grid, ty, tx):
    low = lax.broadcasted_iota(jnp.int32, (8, LANES), 0) < 4
    halves = []
    for jy in (0, 2):
        a = grid[pl.ds(at(ty + 3 * jy, tx), 8, stride=3), :]
        b = grid[pl.ds(at(ty + 3 * jy + 3, tx) - 12, 8, stride=3), :]
        halves.append(jnp.where(low, a, b))
    return jnp.concatenate(halves, axis=0)


def scatter_tile(grid, ty, tx, v):
    for jy in range(4):
        grid[pl.ds(at(ty + 3 * jy, tx), 4, stride=3), :] = v[4 * jy : 4 * jy + 4]


def line(grid, y, x, n, vertical):
    return grid.at[pl.ds(at(y, x), n, stride=PITCH) if vertical else pl.ds(at(y, x), n), :]


def each(n, body):
    def step(k, carry):
        body(k)
        return carry

    lax.fori_loop(0, n, step, 0)


def sample_chunk(k):
    return lax.div(k, CH), lax.rem(k, CH)


SIDES = ((-1, -1, False), (T, -1, False), (0, -1, True), (0, T, True))
SIDE_LEN = (T + 2, T + 2, T, T)


def kernel(
    h_init, c_init, w_hbm, bias, h_seq, c_last,
    w, pt, grid, cgrid, c_own, c_ring, lhs_ring, out_st, h_own, h_ring,
    send_e, send_k, recv_e, recv_k, init_e, init_c, init_k, got_e, got_c, got_k, stage,
    w_sem, out_sem, send_sem, recv_sem, isend_sem, irecv_sem,
):
    rows_n, cols_n = lax.axis_size("rows"), lax.axis_size("cols")
    my_row, my_col = lax.axis_index("rows"), lax.axis_index("cols")

    def exists(d):
        dy, dx = DIRS[d]
        tests = []
        if dy < 0:
            tests.append(my_row > 0)
        if dy > 0:
            tests.append(my_row < rows_n - 1)
        if dx < 0:
            tests.append(my_col > 0)
        if dx > 0:
            tests.append(my_col < cols_n - 1)
        return functools.reduce(jnp.logical_and, tests)

    def peer(d):
        dy, dx = DIRS[d]
        return {"rows": my_row + dy, "cols": my_col + dx}

    for c in range(CH):
        for g in range(4):
            pltpu.make_async_copy(
                w_hbm.at[:, :, :, pl.ds(g * CDIM + c * LANES, LANES)],
                w.at[c, :, :, :, pl.ds(g * LANES, LANES)],
                w_sem.at[c],
            ).start()

    barrier = pltpu.get_barrier_semaphore()
    near = jnp.int32(0)
    for d in range(8):
        near = near + exists(d).astype(jnp.int32)

        @pl.when(exists(d))
        def _():
            pl.semaphore_signal(barrier, inc=1, device_id=peer(d), device_id_type=MESH)

    @functools.partial(each, S * CH)
    def _(k):
        s, c = sample_chunk(k)
        zero = jnp.zeros((GROWS, LANES), jnp.float32)
        grid[0, s, c] = zero
        grid[1, s, c] = zero
        cgrid[s, c] = zero

    @functools.partial(each, S * T)
    def _(k):
        s, y = lax.div(k, T), lax.rem(k, T)
        for c in range(CH):
            lanes = slice(c * LANES, (c + 1) * LANES)
            grid[0, s, c, pl.ds(at(y, 0), T), :] = h_init[s, y, :, lanes].astype(jnp.float32)
            cgrid[s, c, pl.ds(at(y, 0), T), :] = c_init[s, y, :, lanes]

    def edge_line(g, d, depth):
        dy, dx = DIRS[d]
        if dx == 0:
            return line(g, depth if dy < 0 else T - 1 - depth, 0, 16, False)
        return line(g, 0, depth if dx < 0 else T - 1 - depth, 16, True)

    def pack_messages(q, c, b):
        @functools.partial(each, S)
        def _(s):
            for d in range(4):
                send_e[b, d, c, s] = edge_line(grid.at[q, s, c], d, 1)[...].astype(jnp.bfloat16)

        @functools.partial(each, 4)
        def _(k):
            start = at(lax.div(k, 2) * (T - 2), lax.rem(k, 2) * (T - 2))
            for s in range(S):
                stage[k, pl.ds(4 * s, 2), :] = grid[q, s, c, pl.ds(start, 2), :]
                stage[k, pl.ds(4 * s + 2, 2), :] = grid[q, s, c, pl.ds(start + PITCH, 2), :]
            send_k[b, k, c] = stage[k].astype(jnp.bfloat16)

    def message(d, b, slot, sending, c=None):
        e = opposite(d) if sending else d
        if d < 4:
            src, dst = send_e.at[b, d], recv_e.at[slot, e]
        else:
            src, dst = send_k.at[b, d - 4], recv_k.at[slot, e - 4]
        if c is not None:
            src, dst = src.at[c], dst.at[c]
        return pltpu.make_async_remote_copy(
            src_ref=src, dst_ref=dst,
            send_sem=send_sem.at[b, d], recv_sem=recv_sem.at[slot, e],
            device_id=peer(d), device_id_type=MESH,
        )

    def start_messages(c, b, slot):
        for d in range(8):

            @pl.when(exists(d))
            def _():
                message(d, b, slot, True, c).start()

    def take_messages(q, b, slot):
        for d in range(8):

            @pl.when(exists(d))
            def _():
                dy, dx = DIRS[d]
                m = message(d, b, slot, False)
                m.wait_send()
                m.wait_recv()

                @functools.partial(each, CH)
                def _(c):
                    if d < 4:
                        for s in range(S):
                            v = recv_e[slot, d, c, s].astype(jnp.float32)[:T]
                            if dx == 0:
                                line(grid.at[q, s, c], -2 if dy < 0 else T + 1, 0, T, False)[...] = v
                            else:
                                line(grid.at[q, s, c], 0, -2 if dx < 0 else T + 1, T, True)[...] = v
                    else:
                        v = recv_k[slot, d - 4, c].astype(jnp.float32)
                        y0, x0 = (-2 if dy < 0 else T), (-2 if dx < 0 else T)
                        for s in range(S):
                            for k in range(2):
                                grid[q, s, c, pl.ds(at(y0 + k, x0), 2), :] = v[4 * s + 2 * k : 4 * s + 2 * k + 2]

    def init_messages(d, sending):
        e = opposite(d) if sending else d
        if d < 4:
            pairs = ((init_e.at[d], got_e.at[e], 0), (init_c.at[d], got_c.at[e], 1))
        else:
            pairs = ((init_k.at[d - 4], got_k.at[e - 4], 1),)
        return [
            pltpu.make_async_remote_copy(
                src_ref=src, dst_ref=dst,
                send_sem=isend_sem.at[k, d], recv_sem=irecv_sem.at[k, e],
                device_id=peer(d), device_id_type=MESH,
            )
            for src, dst, k in pairs
        ]

    @functools.partial(each, CH)
    def _(c):
        for s in range(S):
            for d in range(4):
                init_e[d, c, s] = edge_line(grid.at[0, s, c], d, 0)[...].astype(jnp.bfloat16)
                init_c[d, c, s] = edge_line(cgrid.at[s, c], d, 0)[...]
        for k in range(4):
            init_k[k, c] = jnp.zeros((8, LANES), jnp.float32)
            for s in range(S):
                start = at((k // 2) * (T - 1), (k % 2) * (T - 1))
                init_k[k, c, pl.ds(s, 1), :] = cgrid[s, c, pl.ds(start, 1), :]
        pack_messages(0, c, 0)

    pl.semaphore_wait(barrier, near)
    for d in range(8):

        @pl.when(exists(d))
        def _():
            for m in init_messages(d, True):
                m.start()
            message(d, 0, 0, True).start()

    for d in range(8):

        @pl.when(exists(d))
        def _():
            dy, dx = DIRS[d]
            for m in init_messages(d, False):
                m.wait_send()
                m.wait_recv()

            @functools.partial(each, CH)
            def _(c):
                for s in range(S):
                    y, x = (-1 if dy < 0 else T if dy > 0 else 0), (-1 if dx < 0 else T if dx > 0 else 0)
                    if d < 4:
                        line(grid.at[0, s, c], y, x, T, dy == 0)[...] = got_e[d, c, s].astype(jnp.float32)[:T]
                        line(cgrid.at[s, c], y, x, T, dy == 0)[...] = got_c[d, c, s][:T]
                    else:
                        cgrid[s, c, pl.ds(at(y, x), 1), :] = got_k[d - 4, c, pl.ds(s, 1), :]

    take_messages(0, 0, 0)

    @functools.partial(each, S * CH)
    def _(k):
        s, c = sample_chunk(k)
        for i in range(9):
            c_own[c, s, i] = gather_tile(cgrid.at[s, c], i // 3, i % 3)
        for k, (y, x, v) in enumerate(SIDES):
            c_ring[c, s, k] = line(cgrid.at[s, c], y, x, 16, v)[...]

    def build_tiles(q, inner):
        @functools.partial(each, S * CH)
        def _(k):
            s, c = sample_chunk(k)
            for ty in range(-1, 4):
                for tx in range(-1, 4):
                    if inner == (0 <= ty < 3 and 0 <= tx < 3):
                        v = gather_tile(grid.at[q, s, c], ty, tx)
                        pt[q, c, s, ty + 1, tx + 1] = v.astype(jnp.bfloat16)

    build_tiles(0, True)
    build_tiles(0, False)

    def ring_ok(k):
        r = lax.broadcasted_iota(jnp.int32, (16, LANES), 0)
        one = r >= 0
        if k == 2:
            return one & (my_col > 0)
        if k == 3:
            return one & (my_col < cols_n - 1)
        sides_ok = ((r > 0) | (my_col > 0)) & ((r < T + 1) | (my_col < cols_n - 1))
        return sides_ok & (one & ((my_row > 0) if k == 0 else (my_row < rows_n - 1)))

    def out_copy(b, t):
        return pltpu.make_async_copy(out_st.at[b], h_seq.at[t], out_sem.at[b])

    def own(t, cur):
        nxt = 1 - cur
        for c in range(CH):
            parts = [
                pt[cur, kc, :, tap // 3 : tap // 3 + 3, tap % 3 : tap % 3 + 3].reshape(S * 144, LANES)
                for tap in range(TAPS)
                for kc in range(CH)
            ]
            lhs = jnp.concatenate(parts, axis=1)
            gates = jnp.dot(lhs, w[c].reshape(TAPS * CDIM, 4 * LANES), preferred_element_type=jnp.float32)
            gates = gates + bias[c, pl.ds(t, 1), :]
            h, cn = lstm(gates, c_own[c].reshape(S * 144, LANES))
            c_own[c] = cn.reshape(S, 9, 16, LANES)
            pt[nxt, c, :, 1:4, 1:4] = h.reshape(S, 3, 3, 16, LANES)
            h_own[...] = h.astype(jnp.float32).reshape(S, 9, 16, LANES)

            @functools.partial(each, S)
            def _(s):
                for i in range(9):
                    scatter_tile(grid.at[nxt, s, c], i // 3, i % 3, h_own[s, i])

            @pl.when(t < STEPS - 2)
            def _():
                pack_messages(nxt, c, nxt)
                start_messages(c, nxt, lax.rem(t + 1, SLOTS))

        @pl.when(t >= 2)
        def _():
            out_copy(nxt, t).wait()

        @functools.partial(each, S * T)
        def _(k):
            s, y = lax.div(k, T), lax.rem(k, T)
            for c in range(CH):
                v = grid[nxt, s, c, pl.ds(at(y, 0), T), :]
                out_st[nxt, s, y, :, c * LANES : (c + 1) * LANES] = v.astype(jnp.bfloat16)

        out_copy(nxt, t).start()

    def ring(t, cur):
        nxt = 1 - cur

        @pl.when(t > 0)
        def _():
            take_messages(cur, cur, lax.rem(t, SLOTS))

        @functools.partial(each, S * CH)
        def _(j):
            s, c = sample_chunk(j)
            for k, (y, x, v) in enumerate(SIDES):
                for tap in range(TAPS):
                    a = line(grid.at[cur, s, c], y + tap // 3 - 1, x + tap % 3 - 1, 16, v)[...]
                    lhs_ring[tap, c, s, k] = a.astype(jnp.bfloat16)

        for c in range(CH):
            parts = [lhs_ring[tap, kc].reshape(S * 64, LANES) for tap in range(TAPS) for kc in range(CH)]
            gates = jnp.dot(
                jnp.concatenate(parts, axis=1),
                w[c].reshape(TAPS * CDIM, 4 * LANES),
                preferred_element_type=jnp.float32,
            )
            gates = gates + bias[c, pl.ds(t, 1), :]
            h, cn = lstm(gates, c_ring[c].reshape(S * 64, LANES))
            c_ring[c] = cn.reshape(S, 4, 16, LANES)
            h_ring[...] = h.astype(jnp.float32).reshape(S, 4, 16, LANES)

            @functools.partial(each, S)
            def _(s):
                for k, (y, x, v) in enumerate(SIDES):
                    m = jnp.where(ring_ok(k), h_ring[s, k], 0.0)
                    line(grid.at[nxt, s, c], y, x, SIDE_LEN[k], v)[...] = m[: SIDE_LEN[k]]

        build_tiles(nxt, False)

    for c in range(CH):
        pltpu.make_async_copy(w_hbm.at[:, :, :, pl.ds(0, 4 * LANES)], w.at[c], w_sem.at[c]).wait()

    @functools.partial(each, STEPS // 2)
    def _(k):
        own(2 * k, 0)
        ring(2 * k, 0)
        own(2 * k + 1, 1)

        @pl.when(k < STEPS // 2 - 1)
        def _():
            ring(2 * k + 1, 1)

    @functools.partial(each, S * CH)
    def _(k):
        s, c = sample_chunk(k)
        for i in range(9):
            scatter_tile(cgrid.at[s, c], i // 3, i % 3, c_own[c, s, i])

    @functools.partial(each, S * T)
    def _(k):
        s, y = lax.div(k, T), lax.rem(k, T)
        for c in range(CH):
            c_last[s, y, :, c * LANES : (c + 1) * LANES] = cgrid[s, c, pl.ds(at(y, 0), T), :]

    out_copy(1, STEPS - 2).wait()
    out_copy(0, STEPS - 1).wait()


def solution(mesh):
    def device_fn(h_init, c_init, w_rec, gate_bias):
        bias = gate_bias.reshape(STEPS, 4, CH, LANES).transpose(2, 0, 1, 3).reshape(CH, STEPS, 4 * LANES)
        vmem = pl.BlockSpec(memory_space=pltpu.VMEM)
        hbm = pl.BlockSpec(memory_space=pl.ANY)
        bf16, f32 = jnp.bfloat16, jnp.float32
        dma = pltpu.SemaphoreType.DMA
        return pl.pallas_call(
            kernel,
            out_shape=(
                jax.ShapeDtypeStruct((STEPS, S, T, T, CDIM), bf16),
                jax.ShapeDtypeStruct((S, T, T, CDIM), f32),
            ),
            in_specs=[vmem, vmem, hbm, vmem],
            out_specs=(hbm, vmem),
            scratch_shapes=[
                pltpu.VMEM((CH, 3, 3, CDIM, 4 * LANES), bf16),
                pltpu.VMEM((2, CH, S, 5, 5, 16, LANES), bf16),
                pltpu.VMEM((2, S, CH, GROWS, LANES), f32),
                pltpu.VMEM((S, CH, GROWS, LANES), f32),
                pltpu.VMEM((CH, S, 9, 16, LANES), f32),
                pltpu.VMEM((CH, S, 4, 16, LANES), f32),
                pltpu.VMEM((TAPS, CH, S, 4, 16, LANES), bf16),
                pltpu.VMEM((2, S, T, T, CDIM), bf16),
                pltpu.VMEM((S, 9, 16, LANES), f32),
                pltpu.VMEM((S, 4, 16, LANES), f32),
                pltpu.VMEM((2, 4, CH, S, 16, LANES), bf16),
                pltpu.VMEM((2, 4, CH, 8, LANES), bf16),
                pltpu.VMEM((SLOTS, 4, CH, S, 16, LANES), bf16),
                pltpu.VMEM((SLOTS, 4, CH, 8, LANES), bf16),
                pltpu.VMEM((4, CH, S, 16, LANES), bf16),
                pltpu.VMEM((4, CH, S, 16, LANES), f32),
                pltpu.VMEM((4, CH, 8, LANES), f32),
                pltpu.VMEM((4, CH, S, 16, LANES), bf16),
                pltpu.VMEM((4, CH, S, 16, LANES), f32),
                pltpu.VMEM((4, CH, 8, LANES), f32),
                pltpu.VMEM((4, 8, LANES), f32),
                dma((CH,)),
                dma((2,)),
                dma((2, 8)),
                dma((SLOTS, 8)),
                dma((2, 8)),
                dma((2, 8)),
            ],
            compiler_params=pltpu.CompilerParams(
                collective_id=0, has_side_effects=True, vmem_limit_bytes=60 * 1024 * 1024
            ),
        )(h_init, c_init, w_rec, bias)

    state_spec = P("dp", "rows", "cols", None)
    return jax.shard_map(
        device_fn,
        mesh=mesh,
        in_specs=(state_spec, state_spec, P(), P()),
        out_specs=(P(None, "dp", "rows", "cols", None), state_spec),
        check_vma=False,
    )
```

time: 406 us -> 113 us (0.28)
  matrix products: 163 us -> 0 us
  starting transfers between devices: 125 us -> 0 us
  Pallas kernels: 0 us -> 97.3 us
  waiting for transfers between devices: 65.6 us -> 0 us
  other arithmetic: 31 us -> 0 us
    conv_general_dilated x12 -> x0, matrix products: 163 us -> none  [one_step(): lax.conv_general_dilated(padded, w_rec, (1, 1), 'VALID', dimension_number...]
    ppermute x48 -> x0, starting transfers between devices: 125 us -> none  [the longest x12 38.9 us: with_halo(): from_left = lax.ppermute(tall_tile[:, :, -1:], 'cols', cols_right)]
    pallas_call x0 -> x1, Pallas kernels: none -> 97.3 us  [device_fn(): pl.pallas_call(kernel, out_shape=(jax.ShapeDtypeStruct((STEPS, S, T, T, C...]
    ppermute x48 -> x0, waiting for transfers between devices: 65.6 us -> none  [the longest x12 34.9 us: with_halo(): from_below = lax.ppermute(tile[:, :1], 'rows', rows_up)]
    dynamic_update_slice x12 -> x0, other arithmetic: 31 us -> none  [device_fn(): final_state, h_seq = lax.scan(one_step, (h_init, c_init), gate_bias)]
    dynamic_slice x12 -> x0, local copies, waits for them, and re-layouts: 9.91 us -> none  [device_fn(): final_state, h_seq = lax.scan(one_step, (h_init, c_init), gate_bias)]
    pallas_call x0 -> x2, local copies, waits for them, and re-layouts: none -> 8.76 us  [device_fn(): pl.pallas_call(kernel, out_shape=(jax.ShapeDtypeStruct((STEPS, S, T, T, C...]
  transfers between devices with their start and end apart: 48 -> 0, of which waited for: 24 -> 0; matrix products, arithmetic and copies ran while one was open for 3% -> 0% of each run, Pallas kernels for 0% -> 0%
where the time goes in v1:
time: 113 us; the launch traced here: 112 us
  Pallas kernels  97.3 us (86%)
  local copies, waits for them, and re-layouts  14 us (12%)
    pallas_call x1, Pallas kernels, device_fn(): pl.pallas_call(kernel, out_shape=(jax.ShapeDtypeStruct((STEPS, S, T, T, C...  97.3 us
    pallas_call x2, local copies, waits for them, and re-layouts, device_fn(): pl.pallas_call(kernel, out_shape=(jax.ShapeDtypeStruct((STEPS, S, T, T, C...  8.76 us
    unnamed x4, local copies, waits for them, and re-layouts  3.57 us

profile of v1, /device:TPU:97, one launch (start us, length us, event | category | flops | bytes accessed | tf_op | source)
XLA Modules:
  0.0 112.0 jit_solution(7208202717542687358)
XLA Ops:
  0.6 1.0 reshape.10
  1.6 0.7 reshape.11.bias
  2.3 1.7 %copy.12.h_init = bf16[2,12,12,384]{3,2,1,0:T(8,128)(2,1)} copy(bf16[2,12,12,384]{3,0,2,1:T(2,128)(2,1)} %param.4) | data formatting | bytes 442368 | tf_op args[0]
  4.0 1.9 %copy.13.c_init = f32[2,12,12,384]{3,2,1,0:T(8,128)} copy(f32[2,12,12,384]{3,0,2,1:T(2,128)} %param.5) | data formatting | bytes 884736 | tf_op args[1]
  5.9 97.3 %shard_map.59 = (bf16[12,2,12,12,384]{4,3,2,1,0:T(8,128)(2,1)}, f32[2,12,12,384]{3,2,1,0:T(8,128)}) custom-call(bf16[2,12,12,384]{3,2,1,0:T(8,128)(2,1)} %copy.12.h_init, f32[2,12,12,384]{3,2,1,0:T(8,128)} %copy.13.c_init, bf16[3,3,384,1536]{3,2,1,0:T(8,128)(2,1)} %w_hbm.1, f32[3,12,512]{2,1,0:T(8,128)} %reshape.11.bias), custom_call_target="tpu_custom_call" | custom-call | tf_op jit(solution)/shard_map/pallas_call | solution.py:408
  103.2 0.0 copy-start
  103.2 7.7 %copy.14 = bf16[12,2,12,12,384]{4,1,3,2,0:T(2,128)(2,1)} copy(bf16[12,2,12,12,384]{4,3,2,1,0:T(8,128)(2,1)} %get-tuple-element.4) | data formatting | bytes 5308416 | tf_op jit(solution)/shard_map/pallas_call | solution.py:408
  110.9 0.0 copy-done
  110.9 1.1 copy.15
  (1 shorter events, 0.0 us)
Async XLA Ops:
  103.2 7.7 %copy-start = (f32[2,12,12,384]{3,2,1,0:T(8,128)S(1)}, f32[2,12,12,384]{3,2,1,0:T(8,128)}, u32[]{:S(2)}) copy-start(f32[2,12,12,384]{3,2,1,0:T(8,128)} %get-tuple-element.5) | copy-start | bytes 1327108

commit v2 on v0

v2 whole, which is shorter than its diff:
```python
import jax
import jax.numpy as jnp
from jax import lax
from jax.experimental import pallas as pl
from jax.experimental.pallas import tpu as pltpu
from jax.sharding import PartitionSpec as P

MESH = pl.DeviceIdType.MESH
STEPS = 12
S = 2
T = 12
LANES = 128
CH = 3
CDIM = CH * LANES
TAPS = 9
KDIM = TAPS * CDIM
SLOTS = 4

YPITCH = 3 * 6 * S
GROWS = 20 * YPITCH
RTILES = 7

DIRS = ((-1, 0), (1, 0), (0, -1), (0, 1), (-1, -1), (-1, 1), (1, -1), (1, 1))


def opposite(d):
    dy, dx = DIRS[d]
    return DIRS.index((-dy, -dx))


def at(y, x):
    return ((y + 2) * 3 + (x + 2) % 3) * 6 * S + (x + 2) // 3 * S


def sigmoid(v):
    return 0.5 * jnp.tanh(0.5 * v) + 0.5


def lstm(gates, bias, c_prev):
    i, f, o, g = (gates[:, k * LANES : (k + 1) * LANES] + bias[k] for k in range(4))
    c = sigmoid(f) * c_prev + sigmoid(i) * jnp.tanh(g)
    h = (sigmoid(o) * jnp.tanh(c)).astype(jnp.bfloat16)
    return h, c


def side_rows(dy):
    return -1 if dy < 0 else T


def ring_rows(g, dy, dx):
    sub = lax.broadcasted_iota(jnp.int32, (8, LANES), 0)
    out = []
    for ix in range(3):
        for y in (-1, T):
            out.append(g[pl.ds(at(y + dy, ix + dx), 8), :])
    for x in (-1, T):
        for s in range(S):
            out.append(g[pl.ds(at(dy, x + dx) + s, 8, stride=YPITCH), :])
    for x in (-1, T):
        a = g[pl.ds(at(8 + dy, x + dx), 8, stride=YPITCH), :]
        b = g[pl.ds(at(4 + dy, x + dx) + 1, 8, stride=YPITCH), :]
        out.append(jnp.where(sub < 4, a, b))
    v = None
    for k, (y, x) in enumerate(((-1, -1), (-1, T), (T, -1), (T, T))):
        a = g[pl.ds(at(y + dy, x + dx) - 2 * k, 8), :]
        v = a if v is None else jnp.where(sub < 2 * k, v, a)
    return out + [v, v]


def put_ring(g, v):
    k = 0
    for ix in range(3):
        for y in (-1, T):
            g[pl.ds(at(y, ix), 8), :] = v[k]
            k += 1
    for x in (-1, T):
        for s in range(S):
            g[pl.ds(at(0, x) + s, 8, stride=YPITCH), :] = v[k]
            k += 1
    for x in (-1, T):
        for s in range(S):
            g[pl.ds(at(8, x) + s, 4, stride=YPITCH), :] = v[k][4 * s : 4 * s + 4]
        k += 1
    for j, (y, x) in enumerate(((-1, -1), (-1, T), (T, -1), (T, T))):
        g[pl.ds(at(y, x), 2), :] = v[k][2 * j : 2 * j + 2]


def put_line(g, d, dist, v):
    dy, dx = DIRS[d]
    if dx == 0:
        y = -dist if dy < 0 else T - 1 + dist
        for ix in range(3):
            g[pl.ds(at(y, ix), 8), :] = v[8 * ix : 8 * ix + 8]
    else:
        x = -dist if dx < 0 else T - 1 + dist
        for k in range(T):
            g[pl.ds(at(6 * (k % 2) + k // 2, x), 2), :] = v[2 * k : 2 * k + 2]


def kernel(
    h_init, c_init, w_hbm, bias_hbm, h_seq, c_last,
    w, bias, pt, grid, cgrid, h_new, c_own, c_ring, lhs_ring,
    recv_v, recv_h, recv_k, first_v, first_h, first_k, firstc_v, firstc_h, firstc_k,
    w_sem, in_sem, out_sem, send_sem, recv_sem, fsend_sem, frecv_sem,
):
    rows_n, cols_n = lax.axis_size("rows"), lax.axis_size("cols")
    my_row, my_col = lax.axis_index("rows"), lax.axis_index("cols")
    f32, bf16 = jnp.float32, jnp.bfloat16

    pt_rows = pt.reshape(CH, 8, 5, 16, LANES)
    own_rows = c_own.reshape(CH, S * T * T, LANES)
    lines = {0: recv_v.reshape(SLOTS, 2, CH, 32, LANES), 1: recv_h.reshape(SLOTS, 2, CH, 32, LANES)}
    corners = recv_k.reshape(SLOTS, 4, CH, 16, LANES)

    def lacks(d):
        dy, dx = DIRS[d]
        r = jnp.bool_(False) if dy == 0 else my_row == (0 if dy < 0 else rows_n - 1)
        c = jnp.bool_(False) if dx == 0 else my_col == (0 if dx < 0 else cols_n - 1)
        return r, c, jnp.logical_or(r, c)

    def flip(v):
        return v + 1 - 2 * lax.rem(v, 2)

    def peer(d, back):
        dy, dx = DIRS[d]
        lr, lc, lack = lacks(d)
        if dx == 0:
            r, c = my_row, flip(my_col)
        elif dy == 0:
            r, c = flip(my_row), my_col
        else:
            a = my_row if dy < 0 else rows_n - 1 - my_row
            b = my_col if dx < 0 else cols_n - 1 - my_col
            on_c = jnp.logical_and(lc, a >= 2)
            on_r = jnp.logical_and(lr, b >= 2)
            if back:
                a3, b3 = jnp.where(a == 1, 0, jnp.where(b == 1, 0, 1)), jnp.where(a == 1, 1, 0)
            else:
                a3, b3 = jnp.where(b == 1, 1, 0), jnp.where(jnp.logical_and(a == 0, b == 0), 1, 0)
            a2 = jnp.where(on_c, flip(a), jnp.where(on_r, 0, a3))
            b2 = jnp.where(on_c, 0, jnp.where(on_r, flip(b), b3))
            r = a2 if dy < 0 else rows_n - 1 - a2
            c = b2 if dx < 0 else cols_n - 1 - b2
        return {"rows": jnp.where(lack, r, my_row + dy), "cols": jnp.where(lack, c, my_col + dx)}

    lack = [lacks(d)[2] for d in range(8)]
    peers = [peer(d, False) for d in range(8)]
    landing = [jnp.where(lack[d], d, opposite(d)) for d in range(8)]

    def kept(d, v):
        return jnp.where(lack[d], jnp.zeros_like(v), v)

    def edge_cells(d, depth):
        dy, dx = DIRS[d]
        if dx == 0:
            return (depth, slice(0, 3), 0, slice(0, 4)) if dy < 0 else (5 - depth, slice(0, 3), 1, slice(0, 4))
        return (slice(0, 6), depth, slice(0, 2), 0) if dx < 0 else (slice(0, 6), 2 - depth, slice(0, 2), 3)

    def corner_cells(d, n):
        dy, dx = DIRS[d]
        iy, jy = (slice(0, n), 0) if dy < 0 else (slice(6 - n, 6), 1)
        ix, jx = (slice(0, n), 0) if dx < 0 else (slice(3 - n, 3), 3)
        return iy, ix, jy, jx

    def moved(i, k):
        return slice(i.start + k, i.stop + k) if isinstance(i, slice) else i + k

    def tile_cells(cells):
        iy, ix, jy, jx = cells
        return pt.at[:, moved(iy, 1), moved(ix, 1), jy, jx]

    def remote(d, src, dst, dst_back, ssem, rsem, rsem_back, sending):
        return pltpu.make_async_remote_copy(
            src_ref=src, dst_ref=dst if sending else dst_back,
            send_sem=ssem, recv_sem=rsem if sending else rsem_back,
            device_id=peers[d], device_id_type=MESH,
        )

    def message(d, slot, sending):
        e = landing[d]
        if d < 2:
            src, dst = tile_cells(edge_cells(d, 1)), lambda k: recv_v.at[slot, k, :, 0:3]
        elif d < 4:
            src, dst = tile_cells(edge_cells(d, 1)), lambda k: recv_h.at[slot, k - 2, :, 0:6]
        else:
            src, dst = tile_cells(corner_cells(d, 2)), lambda k: recv_k.at[slot, k - 4, :, 0:2]
        return remote(
            d, src, dst(e), dst(d), send_sem.at[d], recv_sem.at[slot, e], recv_sem.at[slot, d], sending
        )

    def first_message(d, k, sending):
        e = landing[d]
        cells = edge_cells(d, 0) if d < 4 else corner_cells(d, 1)
        src = tile_cells(cells) if k == 0 else c_own.at[(slice(None),) + cells]
        if d < 2:
            dst = lambda j: (firstc_v if k else first_v).at[j, :, 0:3]
        elif d < 4:
            dst = lambda j: (firstc_h if k else first_h).at[j - 2, :, 0:6]
        else:
            dst = lambda j: (firstc_k if k else first_k).at[j - 4, :, 0:1, 0:1]
        return remote(
            d, src, dst(e), dst(d), fsend_sem.at[k, d], frecv_sem.at[k, e], frecv_sem.at[k, d], sending
        )

    def tile_copy(hbm, vmem, sem, out):
        for c in range(CH):
            for ix in range(3):
                for jy in range(2):
                    a, b = hbm.at[jy, :, :, ix, :, pl.ds(c * LANES, LANES)], vmem(c, ix, jy)
                    pltpu.make_async_copy(b if out else a, a if out else b, sem).start()

    def tile_wait(hbm, vmem, sem, out):
        for c in range(CH):
            for ix in range(3):
                for jy in range(2):
                    a, b = hbm.at[jy, :, :, ix, :, pl.ds(c * LANES, LANES)], vmem(c, ix, jy)
                    pltpu.make_async_copy(b if out else a, a if out else b, sem).wait()

    def h_tiles(c, ix, jy):
        return pt.at[c, 1:7, 1 + ix, jy]

    def c_tiles(c, ix, jy):
        return c_own.at[c, :, ix, jy]

    tile_copy(h_init, h_tiles, in_sem.at[0], False)
    tile_copy(c_init, c_tiles, in_sem.at[1], False)
    bias_copies = [
        pltpu.make_async_copy(bias_hbm.at[:, pl.ds(k * LANES, LANES)], bias.at[k], in_sem.at[2]) for k in range(4 * CH)
    ]
    for m in bias_copies:
        m.start()
    for c in range(CH):
        for kc in range(CH):
            for g in range(4):
                pltpu.make_async_copy(
                    w_hbm.at[:, :, pl.ds(kc * LANES, LANES), pl.ds(g * CDIM + c * LANES, LANES)],
                    w.at[c, kc, :, :, :, pl.ds(g * LANES, LANES)],
                    w_sem.at[c],
                ).start()

    def w_wait(c):
        pltpu.make_async_copy(w.at[c], w.at[c], w_sem.at[c]).wait()

    barrier = pltpu.get_barrier_semaphore()
    for d in range(8):
        pl.semaphore_signal(barrier, inc=1, device_id=peer(d, True), device_id_type=MESH)

    tile_wait(h_init, h_tiles, in_sem.at[0], False)
    pl.semaphore_wait(barrier, 8)
    for d in range(8):
        first_message(d, 0, True).start()
    for d in range(8):
        message(d, 0, True).start()
    tile_wait(c_init, c_tiles, in_sem.at[1], False)
    for d in range(8):
        first_message(d, 1, True).start()
    tile_copy(h_seq.at[STEPS - 1], h_tiles, out_sem, True)

    def put_own(g, hf):
        k = 0
        for iy in range(6):
            for ix in range(3):
                for jy in range(2):
                    g[pl.ds(at(6 * jy + iy, ix), 8), :] = hf[k : k + 8]
                    k += 8

    for c in range(CH):
        put_own(grid.at[c], pt_rows[c, 1:7, 1:4].reshape(S * T * T, LANES).astype(f32))

    def take_first(k, to, gv, gh, gk):
        for d in range(8):
            first_message(d, k, False).wait_recv()
        gv, gh, gk = gv.reshape(2, CH, 32, LANES), gh.reshape(2, CH, 32, LANES), gk.reshape(4, CH, 16, LANES)
        for c in range(CH):
            g = to.at[c]
            for d in range(4):
                v = (gv if d < 2 else gh)[d % 2, c].astype(f32)
                put_line(g, d, 1, kept(d, v[: 2 * T]))
            for d in range(4, 8):
                v = kept(d, gk[d - 4, c].astype(f32)[:8])
                dy, dx = DIRS[d]
                g[pl.ds(at(side_rows(dy), side_rows(dx)), 2), :] = v[:2]

    def build_border(c):
        g = grid.at[c]
        for ty in range(-1, 7):
            for tx in range(-1, 4):
                if not (0 <= ty < 6 and 0 <= tx < 3):
                    v = jnp.concatenate([g[pl.ds(at(ty + 6 * jy, tx), 8), :] for jy in range(2)], axis=0)
                    pt_rows[c, ty + 1, tx + 1] = v.astype(bf16)

    take_first(0, grid, first_v, first_h, first_k)
    for d in range(8):
        first_message(d, 0, False).wait_send()
        first_message(d, 1, False).wait_send()
    for c in range(CH):
        build_border(c)
    for m in bias_copies:
        m.wait()

    def bias_of(t, c):
        return [bias[g * CH + c, pl.ds(t, 1), :] for g in range(4)]

    def own(t, c):
        parts = [
            pt_rows[kc, tap // 3 : tap // 3 + 6, tap % 3 : tap % 3 + 3].reshape(S * T * T, LANES)
            for kc in range(CH)
            for tap in range(TAPS)
        ]
        gates = jnp.dot(
            jnp.concatenate(parts, axis=1), w[c].reshape(KDIM, 4 * LANES), preferred_element_type=f32
        )
        h, cn = lstm(gates, bias_of(t, c), own_rows[c])
        own_rows[c] = cn
        h_new[c] = h

    def take(slot):
        for d in range(8):
            message(d, slot, False).wait_recv()
        for c in range(CH):
            g = grid.at[c]
            for d in range(4):
                put_line(g, d, 2, kept(d, lines[d // 2][slot, d % 2, c].astype(f32)[: 2 * T]))
            for d in range(4, 8):
                v = kept(d, corners[slot, d - 4, c].astype(f32)[:8])
                dy, dx = DIRS[d]
                y0, x0 = (-2 if dy < 0 else T), (-2 if dx < 0 else T)
                for k in range(4):
                    y, x = y0 + k // 2, x0 + k % 2
                    if (y, x) != (side_rows(dy), side_rows(dx)):
                        g[pl.ds(at(y, x), 2), :] = v[2 * k : 2 * k + 2]

    def ring_mask():
        sub = lax.broadcasted_iota(jnp.int32, (8, LANES), 0)
        ok = [jnp.where(lack[d], 0.0, 1.0).astype(f32) for d in range(8)]
        full = lambda v: jnp.full((8, LANES), v, f32)
        out = [full(ok[0]), full(ok[1])] * 3 + [full(ok[2])] * 2 + [full(ok[3])] * 2 + [full(ok[2]), full(ok[3])]
        k = full(ok[7])
        for j in (2, 1, 0):
            k = jnp.where(sub < 2 * (j + 1), full(ok[4 + j]), k)
        return out + [k]

    def ring(t):
        mask = ring_mask()
        for c in range(CH):
            parts = [lhs_ring[kc, tap] for kc in range(CH) for tap in range(TAPS)]
            gates = jnp.dot(
                jnp.concatenate(parts, axis=1), w[c].reshape(KDIM, 4 * LANES), preferred_element_type=f32
            )
            h, cn = lstm(gates, bias_of(t, c), c_ring[c])
            c_ring[c] = cn
            hf = h.astype(f32)
            put_ring(grid.at[c], [hf[8 * k : 8 * k + 8] * m for k, m in enumerate(mask)])
            build_border(c)

    def put_new(t):
        tile_wait(h_seq.at[STEPS - 1], h_tiles, out_sem, True)
        for c in range(CH):
            pt_rows[c, 1:7, 1:4] = h_new[c].reshape(6, 3, 16, LANES)
        tile_copy(h_seq.at[t], h_tiles, out_sem, True)

    def step(t, carry):
        own(t, 1)
        own(t, 2)
        for d in range(8):
            message(d, lax.rem(t, SLOTS), True).wait_send()
        put_new(t)
        for d in range(8):
            message(d, lax.rem(t + 1, SLOTS), True).start()
        take(lax.rem(t, SLOTS))
        for kc in range(CH):
            for tap in range(TAPS):
                v = ring_rows(grid.at[kc], tap // 3 - 1, tap % 3 - 1)
                lhs_ring[kc, tap] = jnp.concatenate(v, axis=0).astype(bf16)
        for c in range(CH):
            put_own(grid.at[c], h_new[c].astype(f32))
        ring(t)
        own(t + 1, 0)
        return carry

    w_wait(0)
    own(0, 0)
    take_first(1, cgrid, firstc_v, firstc_h, firstc_k)
    for c in range(CH):
        c_ring[c] = jnp.concatenate(ring_rows(cgrid.at[c], 0, 0), axis=0)
    w_wait(1)
    w_wait(2)

    lax.fori_loop(0, STEPS - 1, step, 0)
    own(STEPS - 1, 1)
    own(STEPS - 1, 2)
    tile_copy(c_last, c_tiles, in_sem.at[1], True)
    for d in range(8):
        m = message(d, (STEPS - 1) % SLOTS, False)
        m.wait_send()
        m.wait_recv()
    put_new(STEPS - 1)
    tile_wait(h_seq.at[STEPS - 1], h_tiles, out_sem, True)
    tile_wait(c_last, c_tiles, in_sem.at[1], True)


def solution(mesh):
    def device_fn(h_init, c_init, w_rec, gate_bias):
        hbm = pl.BlockSpec(memory_space=pl.ANY)
        bf16, f32 = jnp.bfloat16, jnp.float32
        dma = pltpu.SemaphoreType.DMA
        tiles = (2, 6, 4, 3, S, CDIM)
        h_seq, c_last = pl.pallas_call(
            kernel,
            out_shape=(jax.ShapeDtypeStruct((STEPS,) + tiles, bf16), jax.ShapeDtypeStruct(tiles, f32)),
            in_specs=[hbm] * 4,
            out_specs=(hbm, hbm),
            scratch_shapes=[
                pltpu.VMEM((CH, CH, 3, 3, LANES, 4 * LANES), bf16),
                pltpu.VMEM((4 * CH, STEPS, LANES), f32),
                pltpu.VMEM((CH, 8, 5, 2, 4, S, LANES), bf16),
                pltpu.VMEM((CH, GROWS, LANES), f32),
                pltpu.VMEM((CH, GROWS, LANES), f32),
                pltpu.VMEM((CH, S * T * T, LANES), bf16),
                pltpu.VMEM((CH, 6, 3, 2, 4, S, LANES), f32),
                pltpu.VMEM((CH, RTILES * 16, LANES), f32),
                pltpu.VMEM((CH, TAPS, RTILES * 16, LANES), bf16),
                pltpu.VMEM((SLOTS, 2, CH, 4, 4, S, LANES), bf16),
                pltpu.VMEM((SLOTS, 2, CH, 8, 2, S, LANES), bf16),
                pltpu.VMEM((SLOTS, 4, CH, 4, 2, S, LANES), bf16),
                pltpu.VMEM((2, CH, 4, 4, S, LANES), bf16),
                pltpu.VMEM((2, CH, 8, 2, S, LANES), bf16),
                pltpu.VMEM((4, CH, 4, 2, S, LANES), bf16),
                pltpu.VMEM((2, CH, 4, 4, S, LANES), f32),
                pltpu.VMEM((2, CH, 8, 2, S, LANES), f32),
                pltpu.VMEM((4, CH, 4, 2, S, LANES), f32),
                dma((CH,)),
                dma((3,)),
                dma,
                dma((8,)),
                dma((SLOTS, 8)),
                dma((2, 8)),
                dma((2, 8)),
            ],
            compiler_params=pltpu.CompilerParams(
                collective_id=0, has_side_effects=True, vmem_limit_bytes=60 * 1024 * 1024
            ),
        )(
            h_init.transpose(1, 2, 0, 3).reshape(tiles),
            c_init.transpose(1, 2, 0, 3).reshape(tiles),
            w_rec,
            gate_bias,
        )
        h_seq = h_seq.reshape(STEPS, T, T, S, CDIM).transpose(0, 3, 1, 2, 4)
        return h_seq, c_last.reshape(T, T, S, CDIM).transpose(2, 0, 1, 3)

    state_spec = P("dp", "rows", "cols", None)
    return jax.shard_map(
        device_fn,
        mesh=mesh,
        in_specs=(state_spec, state_spec, P(), P()),
        out_specs=(P(None, "dp", "rows", "cols", None), state_spec),
        check_vma=False,
    )
```

time: 406 us -> 82.7 us (0.20)
  matrix products: 163 us -> 0 us
  starting transfers between devices: 125 us -> 0 us
  Pallas kernels: 0 us -> 75.7 us
  waiting for transfers between devices: 65.6 us -> 0 us
  other arithmetic: 31 us -> 0 us
  local copies, waits for them, and re-layouts: 16.2 us -> 5.89 us
    conv_general_dilated x12 -> x0, matrix products: 163 us -> none  [one_step(): lax.conv_general_dilated(padded, w_rec, (1, 1), 'VALID', dimension_number...]
    ppermute x48 -> x0, starting transfers between devices: 125 us -> none  [the longest x12 38.9 us: with_halo(): from_left = lax.ppermute(tall_tile[:, :, -1:], 'cols', cols_right)]
    pallas_call x0 -> x1, Pallas kernels: none -> 75.7 us  [device_fn(): pl.pallas_call(kernel, out_shape=(jax.ShapeDtypeStruct((STEPS,) + tiles,...]
    ppermute x48 -> x0, waiting for transfers between devices: 65.6 us -> none  [the longest x12 34.9 us: with_halo(): from_below = lax.ppermute(tile[:, :1], 'rows', rows_up)]
    dynamic_update_slice x12 -> x0, other arithmetic: 31 us -> none  [device_fn(): final_state, h_seq = lax.scan(one_step, (h_init, c_init), gate_bias)]
    dynamic_slice x12 -> x0, local copies, waits for them, and re-layouts: 9.91 us -> none  [device_fn(): final_state, h_seq = lax.scan(one_step, (h_init, c_init), gate_bias)]
  transfers between devices with their start and end apart: 48 -> 0, of which waited for: 24 -> 0; matrix products, arithmetic and copies ran while one was open for 3% -> 0% of each run, Pallas kernels for 0% -> 0%
where the time goes in v2:
time: 82.7 us; the launch traced here: 82.2 us
  Pallas kernels  75.7 us (92%)
  local copies, waits for them, and re-layouts  5.89 us (7%)
    pallas_call x1, Pallas kernels, device_fn(): pl.pallas_call(kernel, out_shape=(jax.ShapeDtypeStruct((STEPS,) + tiles,...  75.7 us
    unnamed x4, local copies, waits for them, and re-layouts  5.89 us

profile of v2, /device:TPU:97, one launch (start us, length us, event | category | flops | bytes accessed | tf_op | source)
XLA Modules:
  0.0 82.2 jit_solution(4883523443062077994)
XLA Ops:
  0.6 75.7 %shard_map.59 = (bf16[12,2,6,4,3,2,384]{6,5,4,3,2,1,0:T(2,128)(2,1)}, f32[2,6,4,3,2,384]{5,4,3,2,1,0:T(2,128)}) custom-call(bf16[2,6,4,3,2,384]{5,4,3,2,1,0:T(2,128)(2,1)} %bitcast.15, f32[2,6,4,3,2,384]{5,4,3,2,1,0:T(2,128)} %bitcast.14, bf16[3,3,384,1536]{3,2,1,0:T(8,128)(2,1)} %w_hbm.1, f32[12,1536]{1,0:T(8,128)} %bias_hbm.1), custom_call_target="tpu_custom_call" | custom-call | tf_op jit(solution)/shard_map/pallas_call | solution.py:408
  76.3 0.0 copy-start
  76.3 5.1 %copy.8 = bf16[12,2,12,12,384]{4,1,3,2,0:T(2,128)(2,1)} copy(bf16[12,2,12,12,384]{4,1,3,2,0:T(2,128)(2,1)} %bitcast.12) | data formatting | bytes 5308416
  81.4 0.0 copy-done
  81.5 0.8 copy.9
Async XLA Ops:
  76.3 5.1 %copy-start = (f32[2,6,4,3,2,384]{5,4,3,2,1,0:T(2,128)S(1)}, f32[2,6,4,3,2,384]{5,4,3,2,1,0:T(2,128)}, u32[]{:S(2)}) copy-start(f32[2,6,4,3,2,384]{5,4,3,2,1,0:T(2,128)} %get-tuple-element.5) | copy-start | bytes 1327108

commit v3 on v2

v3 whole, which is shorter than its diff:
```python
import jax
import jax.numpy as jnp
from jax import lax
from jax.experimental import pallas as pl
from jax.experimental.pallas import tpu as pltpu
from jax.sharding import PartitionSpec as P

MESH = pl.DeviceIdType.MESH
STEPS = 12
S = 2
T = 12
LANES = 128
CH = 3
CDIM = CH * LANES
TAPS = 9
KDIM = TAPS * CDIM
SLOTS = 4

YPITCH = 3 * 6 * S
GROWS = 20 * YPITCH
RTILES = 7

DIRS = ((-1, 0), (1, 0), (0, -1), (0, 1), (-1, -1), (-1, 1), (1, -1), (1, 1))


def opposite(d):
    dy, dx = DIRS[d]
    return DIRS.index((-dy, -dx))


def at(y, x):
    return ((y + 2) * 3 + (x + 2) % 3) * 6 * S + (x + 2) // 3 * S


def sigmoid(v):
    return 0.5 * jnp.tanh(0.5 * v) + 0.5


def lstm(gates, bias, c_prev):
    i, f, o, g = (gates[:, k * LANES : (k + 1) * LANES] + bias[k] for k in range(4))
    c = sigmoid(f) * c_prev + sigmoid(i) * jnp.tanh(g)
    h = (sigmoid(o) * jnp.tanh(c)).astype(jnp.bfloat16)
    return h, c


def side_rows(dy):
    return -1 if dy < 0 else T


def ring_rows(g, dy, dx):
    sub = lax.broadcasted_iota(jnp.int32, (8, LANES), 0)
    out = []
    for ix in range(3):
        for y in (-1, T):
            out.append(g[pl.ds(at(y + dy, ix + dx), 8), :])
    for x in (-1, T):
        for s in range(S):
            out.append(g[pl.ds(at(dy, x + dx) + s, 8, stride=YPITCH), :])
    for x in (-1, T):
        a = g[pl.ds(at(8 + dy, x + dx), 8, stride=YPITCH), :]
        b = g[pl.ds(at(4 + dy, x + dx) + 1, 8, stride=YPITCH), :]
        out.append(jnp.where(sub < 4, a, b))
    v = None
    for k, (y, x) in enumerate(((-1, -1), (-1, T), (T, -1), (T, T))):
        a = g[pl.ds(at(y + dy, x + dx) - 2 * k, 8), :]
        v = a if v is None else jnp.where(sub < 2 * k, v, a)
    return out + [v, v]


def put_ring(g, v):
    k = 0
    for ix in range(3):
        for y in (-1, T):
            g[pl.ds(at(y, ix), 8), :] = v[k]
            k += 1
    for x in (-1, T):
        for s in range(S):
            g[pl.ds(at(0, x) + s, 8, stride=YPITCH), :] = v[k]
            k += 1
    for x in (-1, T):
        for s in range(S):
            g[pl.ds(at(8, x) + s, 4, stride=YPITCH), :] = v[k][4 * s : 4 * s + 4]
        k += 1
    for j, (y, x) in enumerate(((-1, -1), (-1, T), (T, -1), (T, T))):
        g[pl.ds(at(y, x), 2), :] = v[k][2 * j : 2 * j + 2]


def lanes(c):
    return slice(c * LANES, (c + 1) * LANES)


def line_pieces(line, c):
    if line.shape[0] == 4:
        return [line[:, ix, :, lanes(c)].reshape(8, LANES) for ix in range(3)]
    return [line[jy, :, :, lanes(c)].reshape(12, LANES) for jy in range(2)]


def put_line(g, d, dist, pieces):
    dy, dx = DIRS[d]
    if dx == 0:
        y = -dist if dy < 0 else T - 1 + dist
        for ix in range(3):
            g[pl.ds(at(y, ix), 8), :] = pieces[ix]
    else:
        x = -dist if dx < 0 else T - 1 + dist
        for jy in range(2):
            for iy in range(6):
                g[pl.ds(at(6 * jy + iy, x), 2), :] = pieces[jy][2 * iy : 2 * iy + 2]


def put_cells(ref, c, v):
    k = 0
    for iy in range(6):
        for ix in range(3):
            for jy in range(2):
                ref[jy, iy, :, ix, :, lanes(c)] = v[k : k + 8].reshape(4, S, LANES)
                k += 8


def get_cells(ref, c):
    return jnp.concatenate(
        [
            ref[jy, iy, :, ix, :, lanes(c)].reshape(8, LANES)
            for iy in range(6)
            for ix in range(3)
            for jy in range(2)
        ],
        axis=0,
    )


def kernel(
    h_init, c_init, w_hbm, bias_hbm, h_seq, c_last,
    w, bias, pt, grid, cgrid, h_new, h_dma, c_own, c_dma, c_ring, lhs_ring,
    recv_v, recv_h, recv_k, first_v, first_h, first_k, firstc_v, firstc_h, firstc_k,
    w_sem, in_sem, out_sem, send_sem, recv_sem, fsend_sem, frecv_sem,
):
    rows_n, cols_n = lax.axis_size("rows"), lax.axis_size("cols")
    my_row, my_col = lax.axis_index("rows"), lax.axis_index("cols")
    f32, bf16 = jnp.float32, jnp.bfloat16

    def lacks(d):
        dy, dx = DIRS[d]
        r = jnp.bool_(False) if dy == 0 else my_row == (0 if dy < 0 else rows_n - 1)
        c = jnp.bool_(False) if dx == 0 else my_col == (0 if dx < 0 else cols_n - 1)
        return r, c, jnp.logical_or(r, c)

    def flip(v):
        return v + 1 - 2 * lax.rem(v, 2)

    def peer(d, back):
        dy, dx = DIRS[d]
        lr, lc, lack = lacks(d)
        if dx == 0:
            r, c = my_row, flip(my_col)
        elif dy == 0:
            r, c = flip(my_row), my_col
        else:
            a = my_row if dy < 0 else rows_n - 1 - my_row
            b = my_col if dx < 0 else cols_n - 1 - my_col
            on_c = jnp.logical_and(lc, a >= 2)
            on_r = jnp.logical_and(lr, b >= 2)
            if back:
                a3, b3 = jnp.where(a == 1, 0, jnp.where(b == 1, 0, 1)), jnp.where(a == 1, 1, 0)
            else:
                a3, b3 = jnp.where(b == 1, 1, 0), jnp.where(jnp.logical_and(a == 0, b == 0), 1, 0)
            a2 = jnp.where(on_c, flip(a), jnp.where(on_r, 0, a3))
            b2 = jnp.where(on_c, 0, jnp.where(on_r, flip(b), b3))
            r = a2 if dy < 0 else rows_n - 1 - a2
            c = b2 if dx < 0 else cols_n - 1 - b2
        return {"rows": jnp.where(lack, r, my_row + dy), "cols": jnp.where(lack, c, my_col + dx)}

    lack = [lacks(d)[2] for d in range(8)]
    peers = [peer(d, False) for d in range(8)]
    landing = [jnp.where(lack[d], d, opposite(d)) for d in range(8)]

    def kept(d, v):
        return jnp.where(lack[d], jnp.zeros_like(v), v)

    def edge_cells(d, depth):
        dy, dx = DIRS[d]
        every = slice(None)
        if dx == 0:
            return (0, depth, every, every) if dy < 0 else (1, 5 - depth, every, every)
        return (every, every, 0, depth) if dx < 0 else (every, every, 3, 2 - depth)

    def corner_cells(d, n):
        dy, dx = DIRS[d]
        jy, iy = (0, slice(0, n)) if dy < 0 else (1, slice(6 - n, 6))
        jx, ix = (0, slice(0, n)) if dx < 0 else (3, slice(3 - n, 3))
        return jy, iy, jx, ix

    def remote(d, src, dst, dst_back, ssem, rsem, rsem_back, sending):
        return pltpu.make_async_remote_copy(
            src_ref=src, dst_ref=dst if sending else dst_back,
            send_sem=ssem, recv_sem=rsem if sending else rsem_back,
            device_id=peers[d], device_id_type=MESH,
        )

    def message(d, slot, sending):
        e = landing[d]
        if d < 2:
            src, dst = h_dma.at[edge_cells(d, 1)], lambda k: recv_v.at[slot, k]
        elif d < 4:
            src, dst = h_dma.at[edge_cells(d, 1)], lambda k: recv_h.at[slot, k - 2]
        else:
            src, dst = h_dma.at[corner_cells(d, 2)], lambda k: recv_k.at[slot, k - 4]
        return remote(
            d, src, dst(e), dst(d), send_sem.at[d], recv_sem.at[slot, e], recv_sem.at[slot, d], sending
        )

    def first_message(d, k, sending):
        e = landing[d]
        cells = edge_cells(d, 0) if d < 4 else corner_cells(d, 1)
        src = (c_dma if k else h_dma).at[cells]
        if d < 2:
            dst = lambda j: (firstc_v if k else first_v).at[j]
        elif d < 4:
            dst = lambda j: (firstc_h if k else first_h).at[j - 2]
        else:
            dst = lambda j: (firstc_k if k else first_k).at[j - 4]
        return remote(
            d, src, dst(e), dst(d), fsend_sem.at[k, d], frecv_sem.at[k, e], frecv_sem.at[k, d], sending
        )

    h_in = pltpu.make_async_copy(h_init, h_dma, in_sem.at[0])
    c_in = pltpu.make_async_copy(c_init, c_dma, in_sem.at[1])
    c_out = pltpu.make_async_copy(c_dma, c_last, in_sem.at[1])

    def h_out(t):
        return pltpu.make_async_copy(h_dma, h_seq.at[t], out_sem)

    h_in.start()
    c_in.start()
    bias_copies = [
        pltpu.make_async_copy(bias_hbm.at[:, pl.ds(k * LANES, LANES)], bias.at[k], in_sem.at[2]) for k in range(4 * CH)
    ]
    for m in bias_copies:
        m.start()
    for c in range(CH):
        for kc in range(CH):
            for g in range(4):
                pltpu.make_async_copy(
                    w_hbm.at[:, :, pl.ds(kc * LANES, LANES), pl.ds(g * CDIM + c * LANES, LANES)],
                    w.at[c, kc, :, :, :, pl.ds(g * LANES, LANES)],
                    w_sem.at[c],
                ).start()

    def w_wait(c):
        pltpu.make_async_copy(w.at[c], w.at[c], w_sem.at[c]).wait()

    barrier = pltpu.get_barrier_semaphore()
    for d in range(8):
        pl.semaphore_signal(barrier, inc=1, device_id=peer(d, True), device_id_type=MESH)

    h_in.wait()
    pl.semaphore_wait(barrier, 8)
    for d in range(8):
        first_message(d, 0, True).start()
    for d in range(8):
        message(d, 0, True).start()
    c_in.wait()
    for d in range(8):
        first_message(d, 1, True).start()
    for c in range(CH):
        c_own[c] = get_cells(c_dma, c)
    h_out(STEPS - 1).start()

    def put_own(g, hf):
        k = 0
        for iy in range(6):
            for ix in range(3):
                for jy in range(2):
                    g[pl.ds(at(6 * jy + iy, ix), 8), :] = hf[k : k + 8]
                    k += 8

    for c in range(CH):
        h = get_cells(h_dma, c)
        pt[c, 1:7, 1:4] = h.reshape(6, 3, 16, LANES)
        put_own(grid.at[c], h.astype(f32))

    def take_first(k, to, gv, gh, gk):
        for d in range(8):
            first_message(d, k, False).wait_recv()
        for c in range(CH):
            g = to.at[c]
            for d in range(4):
                v = line_pieces((gv if d < 2 else gh).at[d % 2], c)
                put_line(g, d, 1, [kept(d, a.astype(f32)) for a in v])
            for d in range(4, 8):
                v = gk[d - 4, 0, 0, :, lanes(c)].astype(f32)
                dy, dx = DIRS[d]
                g[pl.ds(at(side_rows(dy), side_rows(dx)), 2), :] = kept(d, v)

    def build_border(c):
        g = grid.at[c]
        for ty in range(-1, 7):
            for tx in range(-1, 4):
                if not (0 <= ty < 6 and 0 <= tx < 3):
                    v = jnp.concatenate([g[pl.ds(at(ty + 6 * jy, tx), 8), :] for jy in range(2)], axis=0)
                    pt[c, ty + 1, tx + 1] = v.astype(bf16)

    take_first(0, grid, first_v, first_h, first_k)
    for d in range(8):
        first_message(d, 0, False).wait_send()
    for c in range(CH):
        build_border(c)
    for m in bias_copies:
        m.wait()

    def bias_of(t, c):
        return [bias[g * CH + c, pl.ds(t, 1), :] for g in range(4)]

    def own(t, c, lo=0, hi=6):
        n = (hi - lo) * 48
        parts = [
            pt[kc, lo + tap // 3 : hi + tap // 3, tap % 3 : tap % 3 + 3].reshape(n, LANES)
            for kc in range(CH)
            for tap in range(TAPS)
        ]
        gates = jnp.dot(
            jnp.concatenate(parts, axis=1), w[c].reshape(KDIM, 4 * LANES), preferred_element_type=f32
        )
        rows = pl.ds(lo * 48, n)
        h, cn = lstm(gates, bias_of(t, c), c_own[c, rows])
        c_own[c, rows] = cn
        h_new[c, rows] = h

    def take(slot):
        for d in range(8):
            message(d, slot, False).wait_recv()
        for c in range(CH):
            g = grid.at[c]
            for d in range(4):
                v = line_pieces((recv_v if d < 2 else recv_h).at[slot, d % 2], c)
                put_line(g, d, 2, [kept(d, a.astype(f32)) for a in v])
            for d in range(4, 8):
                v = kept(d, recv_k[slot, d - 4, :, :, :, lanes(c)].reshape(8, LANES).astype(f32))
                dy, dx = DIRS[d]
                y0, x0 = (-2 if dy < 0 else T), (-2 if dx < 0 else T)
                for k in range(4):
                    y, x = y0 + k // 2, x0 + k % 2
                    if (y, x) != (side_rows(dy), side_rows(dx)):
                        g[pl.ds(at(y, x), 2), :] = v[2 * k : 2 * k + 2]

    def ring_mask():
        sub = lax.broadcasted_iota(jnp.int32, (8, LANES), 0)
        ok = [jnp.where(lack[d], 0.0, 1.0).astype(f32) for d in range(8)]
        full = lambda v: jnp.full((8, LANES), v, f32)
        out = [full(ok[0]), full(ok[1])] * 3 + [full(ok[2])] * 2 + [full(ok[3])] * 2 + [full(ok[2]), full(ok[3])]
        k = full(ok[7])
        for j in (2, 1, 0):
            k = jnp.where(sub < 2 * (j + 1), full(ok[4 + j]), k)
        return out + [k]

    def ring(t, between):
        mask = ring_mask()
        for c in range(CH):
            parts = [lhs_ring[kc, tap] for kc in range(CH) for tap in range(TAPS)]
            gates = jnp.dot(
                jnp.concatenate(parts, axis=1), w[c].reshape(KDIM, 4 * LANES), preferred_element_type=f32
            )
            if c == 0:
                between()
            h, cn = lstm(gates, bias_of(t, c), c_ring[c])
            c_ring[c] = cn
            hf = h.astype(f32)
            put_ring(grid.at[c], [hf[8 * k : 8 * k + 8] * m for k, m in enumerate(mask)])
            build_border(c)

    def put_new():
        for c in range(CH):
            h = h_new[c]
            put_cells(h_dma, c, h)
            pt[c, 1:7, 1:4] = h.reshape(6, 3, 16, LANES)

    def wait_put(slot):
        for d in range(8):
            message(d, slot, True).wait_send()
        h_out(STEPS - 1).wait()

    def begin(t):
        own(t, 0)
        own(t, 1)
        own(t, 2, 0, 3)

    def step(t, carry):
        wait_put(lax.rem(t, SLOTS))
        take(lax.rem(t, SLOTS))
        for kc in range(CH):
            for tap in range(TAPS):
                v = ring_rows(grid.at[kc], tap // 3 - 1, tap % 3 - 1)
                lhs_ring[kc, tap] = jnp.concatenate(v, axis=0).astype(bf16)
        own(t, 2, 3, 6)
        put_new()

        def send():
            for d in range(8):
                message(d, lax.rem(t + 1, SLOTS), True).start()
            h_out(t).start()
            for c in range(CH):
                put_own(grid.at[c], h_new[c].astype(f32))

        ring(t, send)
        begin(t + 1)
        return carry

    w_wait(0)
    w_wait(1)
    w_wait(2)
    begin(0)
    for d in range(8):
        first_message(d, 1, False).wait_send()
    take_first(1, cgrid, firstc_v, firstc_h, firstc_k)
    for c in range(CH):
        c_ring[c] = jnp.concatenate(ring_rows(cgrid.at[c], 0, 0), axis=0)

    lax.fori_loop(0, STEPS - 1, step, 0)
    wait_put((STEPS - 1) % SLOTS)
    own(STEPS - 1, 2, 3, 6)
    put_new()
    h_out(STEPS - 1).start()
    for c in range(CH):
        put_cells(c_dma, c, c_own[c])
    c_out.start()
    for d in range(8):
        message(d, (STEPS - 1) % SLOTS, False).wait_recv()
    h_out(STEPS - 1).wait()
    c_out.wait()


def copy_out(h, c, h_out, c_out, hv, cv, in_sem, out_sem):
    pieces = [(h.at[t], hv.at[t], h_out.at[t]) for t in range(STEPS)] + [(c, cv, c_out)]
    ins = [pltpu.make_async_copy(a, v, in_sem.at[k]) for k, (a, v, b) in enumerate(pieces)]
    outs = [pltpu.make_async_copy(v, b, out_sem) for a, v, b in pieces]
    for m in ins:
        m.start()
    for m, n in zip(ins, outs):
        m.wait()
        n.start()
    for n in outs:
        n.wait()


def solution(mesh):
    def device_fn(h_init, c_init, w_rec, gate_bias):
        hbm = pl.BlockSpec(memory_space=pl.ANY)
        bf16, f32 = jnp.bfloat16, jnp.float32
        dma = pltpu.SemaphoreType.DMA
        tiles = (2, 6, 4, 3, S, CDIM)
        outs = (jax.ShapeDtypeStruct((STEPS,) + tiles, bf16), jax.ShapeDtypeStruct(tiles, f32))
        state = pl.pallas_call(
            kernel,
            out_shape=outs,
            in_specs=[hbm] * 4,
            out_specs=(hbm, hbm),
            scratch_shapes=[
                pltpu.VMEM((CH, CH, 3, 3, LANES, 4 * LANES), bf16),
                pltpu.VMEM((4 * CH, STEPS, LANES), f32),
                pltpu.VMEM((CH, 8, 5, 16, LANES), bf16),
                pltpu.VMEM((CH, GROWS, LANES), f32),
                pltpu.VMEM((CH, GROWS, LANES), f32),
                pltpu.VMEM((CH, S * T * T, LANES), bf16),
                pltpu.VMEM(tiles, bf16),
                pltpu.VMEM((CH, S * T * T, LANES), f32),
                pltpu.VMEM(tiles, f32),
                pltpu.VMEM((CH, RTILES * 16, LANES), f32),
                pltpu.VMEM((CH, TAPS, RTILES * 16, LANES), bf16),
                pltpu.VMEM((SLOTS, 2, 4, 3, S, CDIM), bf16),
                pltpu.VMEM((SLOTS, 2, 2, 6, S, CDIM), bf16),
                pltpu.VMEM((SLOTS, 4, 2, 2, S, CDIM), bf16),
                pltpu.VMEM((2, 4, 3, S, CDIM), bf16),
                pltpu.VMEM((2, 2, 6, S, CDIM), bf16),
                pltpu.VMEM((4, 1, 1, S, CDIM), bf16),
                pltpu.VMEM((2, 4, 3, S, CDIM), f32),
                pltpu.VMEM((2, 2, 6, S, CDIM), f32),
                pltpu.VMEM((4, 1, 1, S, CDIM), f32),
                dma((CH,)),
                dma((3,)),
                dma,
                dma((8,)),
                dma((SLOTS, 8)),
                dma((2, 8)),
                dma((2, 8)),
            ],
            compiler_params=pltpu.CompilerParams(
                collective_id=0, has_side_effects=True, vmem_limit_bytes=60 * 1024 * 1024
            ),
        )(
            h_init.transpose(1, 2, 0, 3).reshape(tiles),
            c_init.transpose(1, 2, 0, 3).reshape(tiles),
            w_rec,
            gate_bias,
        )
        h_seq, c_last = pl.pallas_call(
            copy_out,
            out_shape=outs,
            in_specs=[hbm] * 2,
            out_specs=(hbm, hbm),
            scratch_shapes=[
                pltpu.VMEM((STEPS,) + tiles, bf16),
                pltpu.VMEM(tiles, f32),
                dma((STEPS + 1,)),
                dma,
            ],
        )(*state)
        h_seq = h_seq.reshape(STEPS, T, T, S, CDIM).transpose(0, 3, 1, 2, 4)
        return h_seq, c_last.reshape(T, T, S, CDIM).transpose(2, 0, 1, 3)

    state_spec = P("dp", "rows", "cols", None)
    return jax.shard_map(
        device_fn,
        mesh=mesh,
        in_specs=(state_spec, state_spec, P(), P()),
        out_specs=(P(None, "dp", "rows", "cols", None), state_spec),
        check_vma=False,
    )
```

time: 82.7 us -> 73.9 us (0.89)
  local copies, waits for them, and re-layouts: 5.89 us -> 0 us
  Pallas kernels: 75.7 us -> 73.1 us
    unnamed x4 -> x0, local copies, waits for them, and re-layouts: 5.89 us -> none
    pallas_call x1 -> x2, Pallas kernels: 75.7 us -> 73.1 us  [the longest x1 70 us: device_fn(): pl.pallas_call(kernel, out_shape=outs, in_specs=[hbm] * 4, out_specs=(hbm...]
where the time goes in v3:
time: 73.9 us; the launch traced here: 73.7 us
  Pallas kernels  73.1 us (99%)
    pallas_call x1, Pallas kernels, device_fn(): pl.pallas_call(kernel, out_shape=outs, in_specs=[hbm] * 4, out_specs=(hbm...  70 us
    pallas_call x1, Pallas kernels, device_fn(): pl.pallas_call(copy_out, out_shape=outs, in_specs=[hbm] * 2, out_specs=(h...  3.09 us

profile of v3, /device:TPU:97, one launch (start us, length us, event | category | flops | bytes accessed | tf_op | source)
XLA Modules:
  0.0 73.7 jit_solution(11797492309702113163)
XLA Ops:
  0.6 70.0 %shard_map.59 = (bf16[12,2,6,4,3,2,384]{6,5,4,3,2,1,0:T(2,128)(2,1)}, f32[2,6,4,3,2,384]{5,4,3,2,1,0:T(2,128)}) custom-call(bf16[2,6,4,3,2,384]{5,4,3,2,1,0:T(2,128)(2,1)} %bitcast.13, f32[2,6,4,3,2,384]{5,4,3,2,1,0:T(2,128)} %bitcast.12, bf16[3,3,384,1536]{3,2,1,0:T(8,128)(2,1)} %w_hbm.1, f32[12,1536]{1,0:T(8,128)} %bias_hbm.1), custom_call_target="tpu_custom_call" | custom-call | tf_op jit(solution)/shard_map/pallas_call | solution.py:452
  70.6 3.1 %shard_map.60 = (bf16[12,2,6,4,3,2,384]{6,5,4,3,2,1,0:T(2,128)(2,1)}, f32[2,6,4,3,2,384]{5,4,3,2,1,0:T(2,128)}) custom-call(bf16[12,2,6,4,3,2,384]{6,5,4,3,2,1,0:T(2,128)(2,1)} %get-tuple-element.6.h, f32[2,6,4,3,2,384]{5,4,3,2,1,0:T(2,128)} %get-tuple-element.7.c), custom_call_target="tpu_custom_call" | custom-call | tf_op jit(solution)/shard_map/pallas_call | solution.py:495

commit v4 on v3

--- a/solution.py
+++ b/solution.py
@@ -130,10 +130,10 @@
 
 
 def kernel(
-    h_init, c_init, w_hbm, bias_hbm, h_seq, c_last,
-    w, bias, pt, grid, cgrid, h_new, h_dma, c_own, c_dma, c_ring, lhs_ring,
+    h_hbm, c_hbm, w_hbm, bias_hbm, h_seq, c_last,
+    h_init, c_init, w, bias, pt, grid, cgrid, h_new, half, c_own, c_ring, lhs_ring,
     recv_v, recv_h, recv_k, first_v, first_h, first_k, firstc_v, firstc_h, firstc_k,
-    w_sem, in_sem, out_sem, send_sem, recv_sem, fsend_sem, frecv_sem,
+    w_sem, bias_sem, in_sem, send_sem, recv_sem, fsend_sem, frecv_sem,
 ):
     rows_n, cols_n = lax.axis_size("rows"), lax.axis_size("cols")
     my_row, my_col = lax.axis_index("rows"), lax.axis_index("cols")
@@ -197,14 +197,14 @@
             device_id=peers[d], device_id_type=MESH,
         )
 
-    def message(d, slot, sending):
+    def message(d, slot, sending, h):
         e = landing[d]
         if d < 2:
-            src, dst = h_dma.at[edge_cells(d, 1)], lambda k: recv_v.at[slot, k]
+            src, dst = h.at[edge_cells(d, 1)], lambda k: recv_v.at[slot, k]
         elif d < 4:
-            src, dst = h_dma.at[edge_cells(d, 1)], lambda k: recv_h.at[slot, k - 2]
+            src, dst = h.at[edge_cells(d, 1)], lambda k: recv_h.at[slot, k - 2]
         else:
-            src, dst = h_dma.at[corner_cells(d, 2)], lambda k: recv_k.at[slot, k - 4]
+            src, dst = h.at[corner_cells(d, 2)], lambda k: recv_k.at[slot, k - 4]
         return remote(
             d, src, dst(e), dst(d), send_sem.at[d], recv_sem.at[slot, e], recv_sem.at[slot, d], sending
         )
@@ -212,7 +212,7 @@
     def first_message(d, k, sending):
         e = landing[d]
         cells = edge_cells(d, 0) if d < 4 else corner_cells(d, 1)
-        src = (c_dma if k else h_dma).at[cells]
+        src = (c_init if k else h_init).at[cells]
         if d < 2:
             dst = lambda j: (firstc_v if k else first_v).at[j]
         elif d < 4:
@@ -223,17 +223,16 @@
             d, src, dst(e), dst(d), fsend_sem.at[k, d], frecv_sem.at[k, e], frecv_sem.at[k, d], sending
         )
 
-    h_in = pltpu.make_async_copy(h_init, h_dma, in_sem.at[0])
-    c_in = pltpu.make_async_copy(c_init, c_dma, in_sem.at[1])
-    c_out = pltpu.make_async_copy(c_dma, c_last, in_sem.at[1])
-
-    def h_out(t):
-        return pltpu.make_async_copy(h_dma, h_seq.at[t], out_sem)
-
+    h_in = pltpu.make_async_copy(h_hbm, h_init, in_sem.at[0])
+    c_in = pltpu.make_async_copy(c_hbm, c_init, in_sem.at[1])
     h_in.start()
     c_in.start()
+    barrier = pltpu.get_barrier_semaphore()
+    for d in range(8):
+        pl.semaphore_signal(barrier, inc=1, device_id=peer(d, True), device_id_type=MESH)
+
     bias_copies = [
-        pltpu.make_async_copy(bias_hbm.at[:, pl.ds(k * LANES, LANES)], bias.at[k], in_sem.at[2]) for k in range(4 * CH)
+        pltpu.make_async_copy(bias_hbm.at[:, pl.ds(k * LANES, LANES)], bias.at[k], bias_sem) for k in range(4 * CH)
     ]
     for m in bias_copies:
         m.start()
@@ -249,22 +248,17 @@
     def w_wait(c):
         pltpu.make_async_copy(w.at[c], w.at[c], w_sem.at[c]).wait()
 
-    barrier = pltpu.get_barrier_semaphore()
-    for d in range(8):
-        pl.semaphore_signal(barrier, inc=1, device_id=peer(d, True), device_id_type=MESH)
-
     h_in.wait()
     pl.semaphore_wait(barrier, 8)
     for d in range(8):
         first_message(d, 0, True).start()
     for d in range(8):
-        message(d, 0, True).start()
+        message(d, 0, True, h_init).start()
     c_in.wait()
     for d in range(8):
         first_message(d, 1, True).start()
     for c in range(CH):
-        c_own[c] = get_cells(c_dma, c)
-    h_out(STEPS - 1).start()
+        c_own[c] = get_cells(c_init, c)
 
     def put_own(g, hf):
         k = 0
@@ -275,7 +269,7 @@
                     k += 8
 
     for c in range(CH):
-        h = get_cells(h_dma, c)
+        h = get_cells(h_init, c)
         pt[c, 1:7, 1:4] = h.reshape(6, 3, 16, LANES)
         put_own(grid.at[c], h.astype(f32))
 
@@ -311,24 +305,25 @@
     def bias_of(t, c):
         return [bias[g * CH + c, pl.ds(t, 1), :] for g in range(4)]
 
-    def own(t, c, lo=0, hi=6):
-        n = (hi - lo) * 48
+    def own_gates(c, lo, hi):
         parts = [
-            pt[kc, lo + tap // 3 : hi + tap // 3, tap % 3 : tap % 3 + 3].reshape(n, LANES)
+            pt[kc, lo + tap // 3 : hi + tap // 3, tap % 3 : tap % 3 + 3].reshape((hi - lo) * 48, LANES)
             for kc in range(CH)
             for tap in range(TAPS)
         ]
-        gates = jnp.dot(
+        return jnp.dot(
             jnp.concatenate(parts, axis=1), w[c].reshape(KDIM, 4 * LANES), preferred_element_type=f32
         )
-        rows = pl.ds(lo * 48, n)
+
+    def own_update(t, c, lo, hi, gates):
+        rows = pl.ds(lo * 48, (hi - lo) * 48)
         h, cn = lstm(gates, bias_of(t, c), c_own[c, rows])
         c_own[c, rows] = cn
         h_new[c, rows] = h
 
     def take(slot):
         for d in range(8):
-            message(d, slot, False).wait_recv()
+            message(d, slot, False, h_init).wait_recv()
         for c in range(CH):
             g = grid.at[c]
             for d in range(4):
@@ -368,36 +363,38 @@
             put_ring(grid.at[c], [hf[8 * k : 8 * k + 8] * m for k, m in enumerate(mask)])
             build_border(c)
 
-    def put_new():
+    def put_new(t):
         for c in range(CH):
             h = h_new[c]
-            put_cells(h_dma, c, h)
+            put_cells(h_seq.at[t], c, h)
             pt[c, 1:7, 1:4] = h.reshape(6, 3, 16, LANES)
 
-    def wait_put(slot):
+    def begin(t):
+        for c in range(2):
+            own_update(t, c, 0, 6, own_gates(c, 0, 6))
+        half[...] = own_gates(2, 0, 3)
+
+    def finish(t):
+        own_update(t, 2, 0, 3, half[...])
+        own_update(t, 2, 3, 6, own_gates(2, 3, 6))
+        put_new(t)
+
+    def sent(slot):
         for d in range(8):
-            message(d, slot, True).wait_send()
-        h_out(STEPS - 1).wait()
-
-    def begin(t):
-        own(t, 0)
-        own(t, 1)
-        own(t, 2, 0, 3)
+            message(d, slot, True, h_init).wait_send()
 
     def step(t, carry):
-        wait_put(lax.rem(t, SLOTS))
+        sent(lax.rem(t, SLOTS))
         take(lax.rem(t, SLOTS))
         for kc in range(CH):
             for tap in range(TAPS):
                 v = ring_rows(grid.at[kc], tap // 3 - 1, tap % 3 - 1)
                 lhs_ring[kc, tap] = jnp.concatenate(v, axis=0).astype(bf16)
-        own(t, 2, 3, 6)
-        put_new()
+        finish(t)
 
         def send():
             for d in range(8):
-                message(d, lax.rem(t + 1, SLOTS), True).start()
-            h_out(t).start()
+                message(d, lax.rem(t + 1, SLOTS), True, h_seq.at[t]).start()
             for c in range(CH):
                 put_own(grid.at[c], h_new[c].astype(f32))
 
@@ -416,54 +413,46 @@
         c_ring[c] = jnp.concatenate(ring_rows(cgrid.at[c], 0, 0), axis=0)
 
     lax.fori_loop(0, STEPS - 1, step, 0)
-    wait_put((STEPS - 1) % SLOTS)
-    own(STEPS - 1, 2, 3, 6)
-    put_new()
-    h_out(STEPS - 1).start()
+    sent((STEPS - 1) % SLOTS)
+    for d in range(8):
+        message(d, (STEPS - 1) % SLOTS, False, h_init).wait_recv()
+    finish(STEPS - 1)
     for c in range(CH):
-        put_cells(c_dma, c, c_own[c])
-    c_out.start()
-    for d in range(8):
-        message(d, (STEPS - 1) % SLOTS, False).wait_recv()
-    h_out(STEPS - 1).wait()
-    c_out.wait()
-
-
-def copy_out(h, c, h_out, c_out, hv, cv, in_sem, out_sem):
-    pieces = [(h.at[t], hv.at[t], h_out.at[t]) for t in range(STEPS)] + [(c, cv, c_out)]
-    ins = [pltpu.make_async_copy(a, v, in_sem.at[k]) for k, (a, v, b) in enumerate(pieces)]
-    outs = [pltpu.make_async_copy(v, b, out_sem) for a, v, b in pieces]
-    for m in ins:
+        put_cells(c_last, c, c_own[c])
+
+
+def copy_out(h, c, h_out, c_out, sem):
+    copies = [pltpu.make_async_copy(h, h_out, sem.at[0]), pltpu.make_async_copy(c, c_out, sem.at[1])]
+    for m in copies:
         m.start()
-    for m, n in zip(ins, outs):
+    for m in copies:
         m.wait()
-        n.start()
-    for n in outs:
-        n.wait()
 
 
 def solution(mesh):
     def device_fn(h_init, c_init, w_rec, gate_bias):
         hbm = pl.BlockSpec(memory_space=pl.ANY)
+        vmem = pl.BlockSpec(memory_space=pltpu.VMEM)
         bf16, f32 = jnp.bfloat16, jnp.float32
         dma = pltpu.SemaphoreType.DMA
         tiles = (2, 6, 4, 3, S, CDIM)
         outs = (jax.ShapeDtypeStruct((STEPS,) + tiles, bf16), jax.ShapeDtypeStruct(tiles, f32))
         state = pl.pallas_call(
             kernel,
-            out_shape=outs,
+            out_shape=tuple(pltpu.VMEM(o.shape, o.dtype) for o in outs),
             in_specs=[hbm] * 4,
-            out_specs=(hbm, hbm),
+            out_specs=(vmem, vmem),
             scratch_shapes=[
+                pltpu.VMEM(tiles, bf16),
+                pltpu.VMEM(tiles, f32),
                 pltpu.VMEM((CH, CH, 3, 3, LANES, 4 * LANES), bf16),
                 pltpu.VMEM((4 * CH, STEPS, LANES), f32),
                 pltpu.VMEM((CH, 8, 5, 16, LANES), bf16),
                 pltpu.VMEM((CH, GROWS, LANES), f32),
                 pltpu.VMEM((CH, GROWS, LANES), f32),
                 pltpu.VMEM((CH, S * T * T, LANES), bf16),
-                pltpu.VMEM(tiles, bf16),
+                pltpu.VMEM((S * T * T // 2, 4 * LANES), f32),
                 pltpu.VMEM((CH, S * T * T, LANES), f32),
-                pltpu.VMEM(tiles, f32),
                 pltpu.VMEM((CH, RTILES * 16, LANES), f32),
                 pltpu.VMEM((CH, TAPS, RTILES * 16, LANES), bf16),
                 pltpu.VMEM((SLOTS, 2, 4, 3, S, CDIM), bf16),
@@ -476,15 +465,15 @@
                 pltpu.VMEM((2, 2, 6, S, CDIM), f32),
                 pltpu.VMEM((4, 1, 1, S, CDIM), f32),
                 dma((CH,)),
-                dma((3,)),
                 dma,
+                dma((2,)),
                 dma((8,)),
                 dma((SLOTS, 8)),
                 dma((2, 8)),
                 dma((2, 8)),
             ],
             compiler_params=pltpu.CompilerParams(
-                collective_id=0, has_side_effects=True, vmem_limit_bytes=60 * 1024 * 1024
+                collective_id=0, has_side_effects=True, vmem_limit_bytes=58 * 1024 * 1024
             ),
         )(
             h_init.transpose(1, 2, 0, 3).reshape(tiles),
@@ -495,14 +484,10 @@
         h_seq, c_last = pl.pallas_call(
             copy_out,
             out_shape=outs,
-            in_specs=[hbm] * 2,
+            in_specs=[vmem] * 2,
             out_specs=(hbm, hbm),
-            scratch_shapes=[
-                pltpu.VMEM((STEPS,) + tiles, bf16),
-                pltpu.VMEM(tiles, f32),
-                dma((STEPS + 1,)),
-                dma,
-            ],
+            scratch_shapes=[dma((2,))],
+            compiler_params=pltpu.CompilerParams(vmem_limit_bytes=16 * 1024 * 1024),
         )(*state)
         h_seq = h_seq.reshape(STEPS, T, T, S, CDIM).transpose(0, 3, 1, 2, 4)
         return h_seq, c_last.reshape(T, T, S, CDIM).transpose(2, 0, 1, 3)

time: 73.9 us -> 72 us (0.974)
  Pallas kernels: 73.1 us -> 71.3 us
    pallas_call x2, Pallas kernels: 73.1 us -> 71.3 us  [the longest x1 69.6 us: device_fn(): pl.pallas_call(kernel, out_shape=tuple((pltpu.VMEM(o.shape, o.dtype) for...]
where the time goes in v4:
time: 72 us; the launch traced here: 71.9 us
  Pallas kernels  71.3 us (99%)
    pallas_call x1, Pallas kernels, device_fn(): pl.pallas_call(kernel, out_shape=tuple((pltpu.VMEM(o.shape, o.dtype) for...  69.6 us
    pallas_call x1, Pallas kernels, device_fn(): pl.pallas_call(copy_out, out_shape=outs, in_specs=[vmem] * 2, out_specs=(...  1.65 us

profile of v4, /device:TPU:97, one launch (start us, length us, event | category | flops | bytes accessed | tf_op | source)
XLA Modules:
  0.0 71.9 jit_solution(3032511887243005766)
XLA Ops:
  0.6 69.6 %shard_map.59 = (bf16[12,2,6,4,3,2,384]{6,5,4,3,2,1,0:T(2,128)(2,1)S(1)}, f32[2,6,4,3,2,384]{5,4,3,2,1,0:T(2,128)S(1)}) custom-call(bf16[2,6,4,3,2,384]{5,4,3,2,1,0:T(2,128)(2,1)} %bitcast.13, f32[2,6,4,3,2,384]{5,4,3,2,1,0:T(2,128)} %bitcast.12, bf16[3,3,384,1536]{3,2,1,0:T(8,128)(2,1)} %w_hbm.1, f32[12,1536]{1,0:T(8,128)} %bias_hbm.1), custom_call_target="tpu_custom_call" | custom-call | tf_op jit(solution)/shard_map/pallas_call | solution.py:440
  70.3 1.7 %shard_map.60 = (bf16[12,2,6,4,3,2,384]{6,5,4,3,2,1,0:T(2,128)(2,1)}, f32[2,6,4,3,2,384]{5,4,3,2,1,0:T(2,128)}) custom-call(bf16[12,2,6,4,3,2,384]{6,5,4,3,2,1,0:T(2,128)(2,1)S(1)} %get-tuple-element.6.h, f32[2,6,4,3,2,384]{5,4,3,2,1,0:T(2,128)S(1)} %get-tuple-element.7.c), custom_call_target="tpu_custom_call" | custom-call | tf_op jit(solution)/shard_map/pallas_call | solution.py:484

commit v5 on v4

--- a/solution.py
+++ b/solution.py
@@ -393,7 +393,7 @@
         finish(t)
 
         def send():
-            for d in range(8):
+            for d in (4, 5, 6, 7, 2, 3, 0, 1):
                 message(d, lax.rem(t + 1, SLOTS), True, h_seq.at[t]).start()
             for c in range(CH):
                 put_own(grid.at[c], h_new[c].astype(f32))

time: 72 us -> 71.5 us (level)
  no operation moved by 1% of the time
where the time goes in v5:
time: 71.5 us; the launch traced here: 71.4 us
  Pallas kernels  70.8 us (99%)
    pallas_call x1, Pallas kernels, device_fn(): pl.pallas_call(kernel, out_shape=tuple((pltpu.VMEM(o.shape, o.dtype) for...  69.1 us
    pallas_call x1, Pallas kernels, device_fn(): pl.pallas_call(copy_out, out_shape=outs, in_specs=[vmem] * 2, out_specs=(...  1.65 us

profile of v5, /device:TPU:97, one launch (start us, length us, event | category | flops | bytes accessed | tf_op | source)
XLA Modules:
  0.0 71.4 jit_solution(13953848784444951320)
XLA Ops:
  0.6 69.1 %shard_map.59 = (bf16[12,2,6,4,3,2,384]{6,5,4,3,2,1,0:T(2,128)(2,1)S(1)}, f32[2,6,4,3,2,384]{5,4,3,2,1,0:T(2,128)S(1)}) custom-call(bf16[2,6,4,3,2,384]{5,4,3,2,1,0:T(2,128)(2,1)} %bitcast.13, f32[2,6,4,3,2,384]{5,4,3,2,1,0:T(2,128)} %bitcast.12, bf16[3,3,384,1536]{3,2,1,0:T(8,128)(2,1)} %w_hbm.1, f32[12,1536]{1,0:T(8,128)} %bias_hbm.1), custom_call_target="tpu_custom_call" | custom-call | tf_op jit(solution)/shard_map/pallas_call | solution.py:440
  69.7 1.7 %shard_map.60 = (bf16[12,2,6,4,3,2,384]{6,5,4,3,2,1,0:T(2,128)(2,1)}, f32[2,6,4,3,2,384]{5,4,3,2,1,0:T(2,128)}) custom-call(bf16[12,2,6,4,3,2,384]{6,5,4,3,2,1,0:T(2,128)(2,1)S(1)} %get-tuple-element.6.h, f32[2,6,4,3,2,384]{5,4,3,2,1,0:T(2,128)S(1)} %get-tuple-element.7.c), custom_call_target="tpu_custom_call" | custom-call | tf_op jit(solution)/shard_map/pallas_call | solution.py:484

commit v6 on v5

--- a/solution.py
+++ b/solution.py
@@ -19,6 +19,10 @@
 YPITCH = 3 * 6 * S
 GROWS = 20 * YPITCH
 RTILES = 7
+ALL = ((0, 6, 0, 3),)
+FIRST, SECOND = ((0, 3, 0, 3),), ((3, 6, 0, 3),)
+INNER = ((1, 5, 1, 2),)
+OUTER = ((0, 6, 0, 1), (0, 6, 2, 3), (0, 1, 1, 2), (5, 6, 1, 2))
 
 DIRS = ((-1, 0), (1, 0), (0, -1), (0, 1), (-1, -1), (-1, 1), (1, -1), (1, 1))
 
@@ -258,7 +262,7 @@
     for d in range(8):
         first_message(d, 1, True).start()
     for c in range(CH):
-        c_own[c] = get_cells(c_init, c)
+        c_own[c] = get_cells(c_init, c).reshape(6, 3, 16, LANES)
 
     def put_own(g, hf):
         k = 0
@@ -294,20 +298,21 @@
                     v = jnp.concatenate([g[pl.ds(at(ty + 6 * jy, tx), 8), :] for jy in range(2)], axis=0)
                     pt[c, ty + 1, tx + 1] = v.astype(bf16)
 
-    take_first(0, grid, first_v, first_h, first_k)
-    for d in range(8):
-        first_message(d, 0, False).wait_send()
-    for c in range(CH):
-        build_border(c)
     for m in bias_copies:
         m.wait()
 
     def bias_of(t, c):
         return [bias[g * CH + c, pl.ds(t, 1), :] for g in range(4)]
 
-    def own_gates(c, lo, hi):
+    def own_gates(c, blocks):
         parts = [
-            pt[kc, lo + tap // 3 : hi + tap // 3, tap % 3 : tap % 3 + 3].reshape((hi - lo) * 48, LANES)
+            jnp.concatenate(
+                [
+                    pt[kc, y0 + tap // 3 : y1 + tap // 3, x0 + tap % 3 : x1 + tap % 3].reshape(-1, LANES)
+                    for y0, y1, x0, x1 in blocks
+                ],
+                axis=0,
+            )
             for kc in range(CH)
             for tap in range(TAPS)
         ]
@@ -315,11 +320,18 @@
             jnp.concatenate(parts, axis=1), w[c].reshape(KDIM, 4 * LANES), preferred_element_type=f32
         )
 
-    def own_update(t, c, lo, hi, gates):
-        rows = pl.ds(lo * 48, (hi - lo) * 48)
-        h, cn = lstm(gates, bias_of(t, c), c_own[c, rows])
-        c_own[c, rows] = cn
-        h_new[c, rows] = h
+    def own_update(t, c, blocks, gates):
+        row = 0
+        for y0, y1, x0, x1 in blocks:
+            shape = y1 - y0, x1 - x0, 16, LANES
+            n = shape[0] * shape[1] * 16
+            h, cn = lstm(gates[row : row + n], bias_of(t, c), c_own[c, y0:y1, x0:x1].reshape(n, LANES))
+            c_own[c, y0:y1, x0:x1] = cn.reshape(shape)
+            h_new[c, y0:y1, x0:x1] = h.reshape(shape)
+            row += n
+
+    def new_rows(c):
+        return h_new[c].reshape(S * T * T, LANES)
 
     def take(slot):
         for d in range(8):
@@ -365,18 +377,18 @@
 
     def put_new(t):
         for c in range(CH):
-            h = h_new[c]
+            h = new_rows(c)
             put_cells(h_seq.at[t], c, h)
             pt[c, 1:7, 1:4] = h.reshape(6, 3, 16, LANES)
 
-    def begin(t):
+    def begin(t, blocks=ALL):
         for c in range(2):
-            own_update(t, c, 0, 6, own_gates(c, 0, 6))
-        half[...] = own_gates(2, 0, 3)
+            own_update(t, c, blocks, own_gates(c, blocks))
+        half[...] = own_gates(2, FIRST)
 
     def finish(t):
-        own_update(t, 2, 0, 3, half[...])
-        own_update(t, 2, 3, 6, own_gates(2, 3, 6))
+        own_update(t, 2, FIRST, half[...])
+        own_update(t, 2, SECOND, own_gates(2, SECOND))
         put_new(t)
 
     def sent(slot):
@@ -396,16 +408,22 @@
             for d in (4, 5, 6, 7, 2, 3, 0, 1):
                 message(d, lax.rem(t + 1, SLOTS), True, h_seq.at[t]).start()
             for c in range(CH):
-                put_own(grid.at[c], h_new[c].astype(f32))
+                put_own(grid.at[c], new_rows(c).astype(f32))
 
         ring(t, send)
         begin(t + 1)
         return carry
 
-    w_wait(0)
-    w_wait(1)
+    for c in range(2):
+        w_wait(c)
+        own_update(0, c, INNER, own_gates(c, INNER))
+    take_first(0, grid, first_v, first_h, first_k)
+    for d in range(8):
+        first_message(d, 0, False).wait_send()
+    for c in range(CH):
+        build_border(c)
     w_wait(2)
-    begin(0)
+    begin(0, OUTER)
     for d in range(8):
         first_message(d, 1, False).wait_send()
     take_first(1, cgrid, firstc_v, firstc_h, firstc_k)
@@ -418,7 +436,7 @@
         message(d, (STEPS - 1) % SLOTS, False, h_init).wait_recv()
     finish(STEPS - 1)
     for c in range(CH):
-        put_cells(c_last, c, c_own[c])
+        put_cells(c_last, c, c_own[c].reshape(S * T * T, LANES))
 
 
 def copy_out(h, c, h_out, c_out, sem):
@@ -450,9 +468,9 @@
                 pltpu.VMEM((CH, 8, 5, 16, LANES), bf16),
                 pltpu.VMEM((CH, GROWS, LANES), f32),
                 pltpu.VMEM((CH, GROWS, LANES), f32),
-                pltpu.VMEM((CH, S * T * T, LANES), bf16),
+                pltpu.VMEM((CH, 6, 3, 16, LANES), bf16),
                 pltpu.VMEM((S * T * T // 2, 4 * LANES), f32),
-                pltpu.VMEM((CH, S * T * T, LANES), f32),
+                pltpu.VMEM((CH, 6, 3, 16, LANES), f32),
                 pltpu.VMEM((CH, RTILES * 16, LANES), f32),
                 pltpu.VMEM((CH, TAPS, RTILES * 16, LANES), bf16),
                 pltpu.VMEM((SLOTS, 2, 4, 3, S, CDIM), bf16),

time: 71.5 us -> 71.1 us (level)
  no operation moved by 1% of the time
where the time goes in v6:
time: 71.1 us; the launch traced here: 71 us
  Pallas kernels  70.3 us (99%)
    pallas_call x1, Pallas kernels, device_fn(): pl.pallas_call(kernel, out_shape=tuple((pltpu.VMEM(o.shape, o.dtype) for...  68.7 us
    pallas_call x1, Pallas kernels, device_fn(): pl.pallas_call(copy_out, out_shape=outs, in_specs=[vmem] * 2, out_specs=(...  1.65 us

profile of v6, /device:TPU:97, one launch (start us, length us, event | category | flops | bytes accessed | tf_op | source)
XLA Modules:
  0.0 71.0 jit_solution(18241772682835749049)
XLA Ops:
  0.6 68.7 %shard_map.59 = (bf16[12,2,6,4,3,2,384]{6,5,4,3,2,1,0:T(2,128)(2,1)S(1)}, f32[2,6,4,3,2,384]{5,4,3,2,1,0:T(2,128)S(1)}) custom-call(bf16[2,6,4,3,2,384]{5,4,3,2,1,0:T(2,128)(2,1)} %bitcast.13, f32[2,6,4,3,2,384]{5,4,3,2,1,0:T(2,128)} %bitcast.12, bf16[3,3,384,1536]{3,2,1,0:T(8,128)(2,1)} %w_hbm.1, f32[12,1536]{1,0:T(8,128)} %bias_hbm.1), custom_call_target="tpu_custom_call" | custom-call | tf_op jit(solution)/shard_map/pallas_call | solution.py:458
  69.3 1.7 %shard_map.60 = (bf16[12,2,6,4,3,2,384]{6,5,4,3,2,1,0:T(2,128)(2,1)}, f32[2,6,4,3,2,384]{5,4,3,2,1,0:T(2,128)}) custom-call(bf16[12,2,6,4,3,2,384]{6,5,4,3,2,1,0:T(2,128)(2,1)S(1)} %get-tuple-element.6.h, f32[2,6,4,3,2,384]{5,4,3,2,1,0:T(2,128)S(1)} %get-tuple-element.7.c), custom_call_target="tpu_custom_call" | custom-call | tf_op jit(solution)/shard_map/pallas_call | solution.py:502
